TPU v7x, 32 devices: a whole 2x2x4 slice. The times are simulated.
32 devices in a mesh: variant: 4 (over x, core), mesh: 8 (over z, y).
Axes of the slice: x: 2, y: 2, z: 4, core: 2. Of those that a mesh axis runs over, the one named last changes fastest.
Arguments:
- snapshots: float32 [4, 64, 131072], P('variant', None, 'mesh'), may hold values from -12 to 12, as said below
- ref_index: int32 [1], replicated, may hold values from 0 to 3
- weight_codes: int32 [4], replicated, may hold values from 1 to 16
Outputs:
- new_basis: float32 [64, 131072], P(None, 'mesh')
Inputs may be any that keep to these rules, and one draw needn't show every extreme that they name: `snapshots`: each variant's snapshot matrix has full rank 64, and the principal angles between any two variants' spans have tangents below 0.8.
All inputs are finite; a program needn't handle non-finite values.
Results may differ from a plain program's by a relative error of at most 0.0001.
Values sent between devices are 32-bit elements; how exact they have to be, the bound alone decides.
No kernel may reach another device: no remote copies, remote signals or barrier semaphores. Data moves between devices by JAX's collectives and lax.ppermute only.
A program may use at most 64 MiB of HBM per device.

v0:
```python
import math

import jax
import jax.numpy as jnp
from jax import lax
from jax.sharding import PartitionSpec as P

highest = lax.Precision.HIGHEST
atan_coeffs = [(-1.0) ** k / (2 * k + 1) for k in range(24)]
cos_coeffs = [(-1.0) ** k / math.factorial(2 * k) for k in range(24)]
sin_coeffs = [(-1.0) ** k / math.factorial(2 * k + 1) for k in range(24)]


def broadcast(x, axis, root):
    mine = lax.axis_index(axis) == root
    return lax.psum(jnp.where(mine, x, jnp.zeros_like(x)), axis)


def product(left, right):
    return jnp.dot(left, right, precision=highest, preferred_element_type=jnp.float32)


def series(matrix, coeffs):
    eye = jnp.eye(matrix.shape[0], dtype=jnp.float32)
    total = coeffs[-1] * eye
    for coeff in reversed(coeffs[:-1]):
        total = coeff * eye + product(matrix, total)
    return total


def inverse(matrix):
    factor = jnp.linalg.cholesky(product(matrix.T, matrix))
    return jax.scipy.linalg.cho_solve((factor, True), matrix.T)


def on_device(snapshots, ref_index, weight_codes):
    own_snap = snapshots[0]
    root = ref_index[0]
    codes = weight_codes.astype(jnp.float32)
    weight = codes[lax.axis_index("variant")] / jnp.sum(codes)
    eye = jnp.eye(own_snap.shape[0], dtype=jnp.float32)
    scale = jnp.float32(math.sqrt(own_snap.shape[1] * lax.axis_size("mesh")))
    gram_own = lax.psum(product(own_snap, own_snap.T), "mesh")
    lower_own = jnp.linalg.cholesky(gram_own)
    base_own = jax.scipy.linalg.solve_triangular(lower_own, own_snap, lower=True)
    base_ref = broadcast(base_own, "variant", root)
    correlation = lax.psum(product(base_ref, base_own.T), "mesh")
    minv = inverse(correlation)
    tangent = product(minv.T, base_own) - base_ref
    tangent_gram = product(minv.T, minv) - eye
    term = weight * product(series(tangent_gram, atan_coeffs), tangent)
    blended = lax.psum(term, "variant")
    energy = lax.psum(product(blended, blended.T), "mesh")
    mixed = product(series(energy, cos_coeffs), base_ref) + product(
        series(energy, sin_coeffs), blended
    )
    return mixed * scale


def solution(mesh):
    return jax.shard_map(
        on_device,
        mesh=mesh,
        in_specs=(P("variant", None, "mesh"), P(), P()),
        out_specs=P(None, "mesh"),
        check_vma=False,
    )
```

profile of v0, /device:TPU:0, one launch (start us, length us, event | category | flops | bytes accessed | tf_op | source)
XLA Modules:
  0.0 382.1 jit_solution(7541241715108822365)
XLA Ops:
  6.5 6.9 %fusion.3 = f32[64,64]{0,1:T(8,128)S(1)} fusion(f32[1,64,16384]{2,1,0:T(8,128)} %param.4), kind=kOutput, calls=%fused_computation.6 | convolution fusion | flops 805306368 | bytes 4210688 | tf_op jit(solution)/shard_map/dot_general | solution.py:20
  13.5 38.9 %psum.35 = f32[64,64]{0,1:T(8,128)S(1)} all-reduce(f32[64,64]{0,1:T(8,128)S(1)} %fusion.3), channel_id=1, replica_groups=mesh['variant'=4,'mesh'=8] {'mesh'}, use_global_device_ids=true, to_apply=%region_1.0 | all-reduce | flops 4096 | bytes 32768 | tf_op jit(solution)/shard_map/psum | solution.py:43
  52.5 5.8 %cholesky.44 = f32[64,64]{1,0:T(8,128)S(1)} custom-call(f32[64,64]{1,0:T(8,128)S(1)} %fusion.15), custom_call_target="Cholesky" | custom-call | tf_op jit(solution)/shard_map/jit(cholesky)/cholesky | solution.py:44
  58.4 0.6 compare_reduce_fusion.1
  59.0 0.7 fusion.7
  59.7 4.9 %custom-call.13 = f32[1,64,64]{1,2,0:T(8,128)S(1)} custom-call(f32[1,64,64]{2,1,0:T(8,128)S(1)} %fusion.7), custom_call_target="InvertDiagBlocksLowerTriangular" | custom-call | tf_op jit(solution)/shard_map/jit(_solve_triangular)/triangular_solve | solution.py:45
  65.2 9.3 %broadcast_select_fusion = (f32[64,16384]{1,0:T(8,128)}, f32[64,16384]{1,0:T(8,128)}) fusion(pred[]{:T(512)S(6)} %eq.142, f32[1,64,16384]{2,1,0:T(8,128)} %param.4, f32[1,64,64]{1,2,0:T(8,128)S(1)} %custom-call.13), kind=kOutput, calls=%fused_computation.8 | convolution fusion | flops 806354944 | bytes 12599297 | tf_op jit(solution)/shard_map/jit(_solve_triangular)/triangular_solve | solution.py:45
  74.5 0.2 all-reduce.5.cloned.1.call-start
  74.8 0.4 copy-done.1
  75.2 0.6 dynamic_slice.3
  75.7 0.6 convert_reduce_fusion
  77.6 79.8 %all-reduce.3.cloned.1.call-done = f32[64,16384]{1,0:T(8,128)} async-done(((f32[64,16384]{1,0:T(8,128)}), f32[64,16384]{1,0:T(8,128)}) %all-reduce.3.cloned.1.call-update) | async-done | bytes 4194320 | tf_op jit(solution)/shard_map/psum | solution.py:16
  157.4 6.9 %fusion.35 = f32[64,64]{1,0:T(8,128)S(1)} fusion(f32[64,16384]{1,0:T(8,128)} %all-reduce.3.cloned.1.call-done, f32[64,16384]{1,0:T(8,128)} %get-tuple-element.7), kind=kOutput, calls=%fused_computation.114 | convolution fusion | flops 805306368 | bytes 8404992 | tf_op jit(solution)/shard_map/dot_general | solution.py:20
  164.4 37.1 %psum.37 = f32[64,64]{1,0:T(8,128)S(1)} all-reduce(f32[64,64]{1,0:T(8,128)S(1)} %fusion.35), channel_id=1, replica_groups=mesh['variant'=4,'mesh'=8] {'mesh'}, use_global_device_ids=true, to_apply=%region_5.7 | all-reduce | flops 4096 | bytes 32768 | tf_op jit(solution)/shard_map/psum | solution.py:47
  201.5 0.2 fusion.36
  201.8 5.8 %cholesky.55 = f32[64,64]{1,0:T(8,128)S(1)} custom-call(f32[64,64]{1,0:T(8,128)S(1)} %fusion.13), custom_call_target="Cholesky" | custom-call | tf_op jit(solution)/shard_map/jit(cholesky)/cholesky | solution.py:32
  207.7 0.6 compare_reduce_fusion
  208.3 0.7 fusion.8
  209.0 4.9 %custom-call.14 = f32[1,64,64]{1,2,0:T(8,128)S(1)} custom-call(f32[1,64,64]{2,1,0:T(8,128)S(1)} %fusion.8), custom_call_target="InvertDiagBlocksLowerTriangular" | custom-call | tf_op jit(solution)/shard_map/jit(_cho_solve)/triangular_solve | solution.py:33
  213.9 0.2 fusion.11
  214.3 0.2 convolution_subtract_fusion.1
  214.5 0.2 convolution_add_fusion.62
  215.2 0.2 convolution_add_fusion.58
  215.4 0.2 convolution_add_fusion.57
  215.9 0.2 convolution_add_fusion.54
  216.8 0.2 convolution_add_fusion.49
  216.9 0.2 convolution_add_fusion.48
  217.8 0.2 convolution_add_fusion.43
  218.3 0.2 convolution_add_fusion.40
  218.5 7.2 %convolution_subtract_fusion = f32[64,16384]{1,0:T(8,128)S(1)} fusion(f32[64,16384]{1,0:T(8,128)} %all-reduce.3.cloned.1.call-done, f32[64,64]{1,0:T(8,128)S(1)} %fusion.9, f32[64,16384]{1,0:T(8,128)} %get-tuple-element.7), kind=kOutput, calls=%fused_computation.3 | convolution fusion | flops 806354944 | bytes 12599296 | tf_op jit(solution)/shard_map/dot_general | solution.py:20
  225.7 5.2 %convolution_multiply_fusion = f32[64,16384]{1,0:T(8,128)} fusion(f32[64,64]{1,0:T(8,128)S(1)} %convolution_add_fusion.40, f32[64,16384]{1,0:T(8,128)S(1)} %convolution_subtract_fusion, f32[]{:T(128)S(6)} %div.9), kind=kOutput, calls=%fused_computation.2 | convolution fusion | flops 806354944 | bytes 8404996 | tf_op jit(solution)/shard_map/dot_general | solution.py:20
  230.9 82.1 %all-reduce.5.cloned.1.call-done = f32[64,16384]{1,0:T(8,128)} async-done(((f32[64,16384]{1,0:T(8,128)}), f32[64,16384]{1,0:T(8,128)}) %all-reduce.5.cloned.1.call-update) | async-done | bytes 4194320 | tf_op jit(solution)/shard_map/psum | solution.py:52
  313.0 6.9 %fusion.37 = f32[64,64]{1,0:T(8,128)S(1)} fusion(f32[64,16384]{1,0:T(8,128)} %all-reduce.5.cloned.1.call-done), kind=kOutput, calls=%fused_computation.116 | convolution fusion | flops 805306368 | bytes 4210688 | tf_op jit(solution)/shard_map/dot_general | solution.py:20
  320.0 37.1 %psum.39 = f32[64,64]{1,0:T(8,128)S(1)} all-reduce(f32[64,64]{1,0:T(8,128)S(1)} %fusion.37), channel_id=1, replica_groups=mesh['variant'=4,'mesh'=8] {'mesh'}, use_global_device_ids=true, to_apply=%region_7.9 | all-reduce | flops 4096 | bytes 32768 | tf_op jit(solution)/shard_map/psum | solution.py:53
  357.1 0.2 fusion.5
  357.7 0.2 convolution_add_fusion.19
  357.9 0.2 convolution_add_fusion.38
  358.6 0.2 convolution_add_fusion.15
  359.1 0.2 convolution_add_fusion.12
  360.0 0.2 convolution_add_fusion.7
  360.1 0.2 convolution_add_fusion.6
  361.0 0.2 convolution_add_fusion.1
  361.5 0.2 convolution_add_fusion.35
  362.3 0.2 convolution_add_fusion.30
  362.5 0.2 convolution_add_fusion.29
  363.9 0.2 convolution_add_fusion.21
  364.2 5.6 %fusion.40 = f32[64,16384]{1,0:T(8,128)S(1)} fusion(f32[64,64]{1,0:T(8,128)S(1)} %convolution_add_fusion.20, f32[64,16384]{1,0:T(8,128)} %all-reduce.3.cloned.1.call-done), kind=kOutput, calls=%fused_computation.119 | convolution fusion | flops 805306368 | bytes 8404992 | tf_op jit(solution)/shard_map/dot_general | solution.py:20
  369.9 5.4 %fusion = f32[64,16384]{1,0:T(8,128)} fusion(f32[64,16384]{1,0:T(8,128)S(1)} %fusion.40, f32[64,64]{1,0:T(8,128)S(1)} %convolution_add_fusion.1, f32[64,16384]{1,0:T(8,128)S(1)} %copy-done), kind=kOutput, calls=%fused_computation.1 | convolution fusion | flops 807403520 | bytes 12599296 | tf_op jit(solution)/shard_map/dot_general | solution.py:20
  (59 shorter events, 7.7 us)
Async XLA Ops:
  6.5 150.9 %all-reduce.3.cloned.1.call-start = ((), (), s32[]{:S(2)}) async-start(), calls=%async_computation | async-start | bytes 8388608 | tf_op jit(solution)/shard_map/psum | solution.py:16
  74.5 0.7 copy-start.1
  74.5 238.5 %all-reduce.5.cloned.1.call-start = ((), (), s32[]{:S(2)}) async-start(), calls=%async_computation.1 | async-start | bytes 8388608 | tf_op jit(solution)/shard_map/psum | solution.py:52
  364.2 5.6 %copy-start = (f32[64,16384]{1,0:T(8,128)S(1)}, f32[64,16384]{1,0:T(8,128)}, u32[]{:S(2)}) copy-start(f32[64,16384]{1,0:T(8,128)} %all-reduce.5.cloned.1.call-done) | copy-start | bytes 12582916
Sparse Core Ops, SparseCore 0:
  74.7 82.7 all-reduce.2
  231.0 81.9 all-reduce.4
where the time goes:
time: 382 us
  waiting for transfers between devices  162 us (42%)
  blocking collectives  113 us (30%)
  matrix products  64.9 us (17%)
  other arithmetic  24.8 us (6%)
  between operations  15.9 us (4%)
    psum x1, waiting for transfers between devices, on_device(): blended = lax.psum(term, 'variant')  82.1 us
    psum x1, waiting for transfers between devices, broadcast(): return lax.psum(jnp.where(mine, x, jnp.zeros_like(x)), axis)  79.8 us
    dot_general x74, matrix products, product(): jnp.dot(left, right, precision=highest, preferred_element_type=jnp.float32)  55.2 us
    psum x1, blocking collectives, on_device(): gram_own = lax.psum(product(own_snap, own_snap.T), 'mesh')  38.9 us
    psum x1, blocking collectives, on_device(): correlation = lax.psum(product(base_ref, base_own.T), 'mesh')  37.1 us
    psum x1, blocking collectives, on_device(): energy = lax.psum(product(blended, blended.T), 'mesh')  37.1 us
    another operation x1, matrix products, on_device(): jax.scipy.linalg.solve_triangular(lower_own, own_snap, lower=True)  9.28 us
  transfers between devices with their start and end apart: 2, of which 2 were waited for; matrix products, arithmetic and copies ran while one was open for 0% of the time, Pallas kernels for 0%

commit v1 on v0

v1 whole, which is shorter than its diff:
```python
import functools
import math

import jax
import jax.numpy as jnp
from jax import lax
from jax.experimental import pallas as pl
from jax.experimental.pallas import tpu as pltpu
from jax.sharding import PartitionSpec as P


highest = lax.Precision.HIGHEST
atan_coeffs = [(-1.0) ** k / (2 * k + 1) for k in range(24)]
cos_coeffs = [(-1.0) ** k / math.factorial(2 * k) for k in range(24)]
sin_coeffs = [(-1.0) ** k / math.factorial(2 * k + 1) for k in range(24)]

CORES = 2
LOWEST = 1.0 / 1.64
STEP = 6


def xor_pairs(size, offset):
    return [(i, i ^ offset) for i in range(size)]


def mm(a, b):
    return jnp.dot(a, b, precision=highest, preferred_element_type=jnp.float32)


def mmt(a, b):
    return lax.dot_general(
        a, b, (((1,), (1,)), ((), ())), precision=highest, preferred_element_type=jnp.float32
    )


def powers_of(matrix, top):
    powers = {1: matrix}
    for k in range(2, top + 1):
        powers[k] = mm(powers[k // 2], powers[k - k // 2])
    return powers


def split(x):
    high = x.astype(jnp.bfloat16)
    rest = x - high.astype(jnp.float32)
    middle = rest.astype(jnp.bfloat16)
    low = (rest - middle.astype(jnp.float32)).astype(jnp.bfloat16)
    return high, middle, low


def raw_gram(a, b):
    return lax.dot_general(a, b, (((1,), (1,)), ((), ())), preferred_element_type=jnp.float32)


def fold(total, rows):
    tall = total.shape[0] // 3
    part = lambda i, j: total[i * tall:(i + 1) * tall, j * rows:(j + 1) * rows]
    order = sorted(((i, j) for i in range(3) for j in range(3)), key=lambda ij: -sum(ij))
    result = part(*order[0])
    for ij in order[1:]:
        result = result + part(*ij)
    return result


def gram_kernel(heads, groups, prior, where, *refs):
    count = heads + max(groups) + (1 if prior else 0)
    refs_in, out, totals = refs[:count], refs[count], refs[count + 1:]
    step, last = pl.program_id(0), pl.num_programs(0) - 1
    cols = refs_in[heads:heads + max(groups)]
    size = cols[0].shape[0]
    pieces = [split(col[...]) for col in cols]

    @pl.when(step == 0)
    def _():
        for total in totals:
            total[...] = jnp.zeros_like(total)

    for head in range(heads):
        right = jnp.concatenate(split(refs_in[head][...]), axis=0)
        left = jnp.concatenate(
            [pieces[g][level] for level in range(3) for g in range(groups[head])], axis=0
        )
        totals[head][...] += raw_gram(left, right)

    @pl.when(step == last)
    def _():
        blocks = []
        for head in range(heads):
            result = fold(totals[head][...], size)
            blocks += [result[g * size:(g + 1) * size] for g in range(groups[head])]
        result = jnp.concatenate(blocks, axis=1)
        out[...] = result + refs_in[count - 1][...] if prior else result


def gram(place, heads, whole, cols, groups, before, extent, tile):
    size = whole[0].shape[0]
    tile = min(tile, extent)
    steps = extent // tile
    width = sum(groups) * size
    at_place = pl.BlockSpec((size, tile), lambda i, w: (0, w[0] * steps + i))
    at_start = pl.BlockSpec((size, tile), lambda i, w: (0, i))
    block = pl.BlockSpec((size, width), lambda i, w: (0, 0))
    operands = [*heads, *whole, *cols]
    specs = [at_start] * len(heads) + [at_place] * len(whole) + [at_start] * len(cols)
    if before is not None:
        operands.append(before)
        specs.append(block)
    return pl.pallas_call(
        functools.partial(gram_kernel, len(heads), groups, before is not None),
        out_shape=jax.ShapeDtypeStruct((size, width), jnp.float32),
        grid_spec=pltpu.PrefetchScalarGridSpec(
            num_scalar_prefetch=1,
            grid=(steps,),
            in_specs=specs,
            out_specs=block,
            scratch_shapes=[pltpu.VMEM((3 * g * size, 3 * size), jnp.float32) for g in groups],
        ),
        cost_estimate=pl.CostEstimate(
            flops=9 * 2 * size * width * extent, transcendentals=0,
            bytes_accessed=4 * (len(operands)) * size * extent,
        ),
    )(place, *operands)


def diagonal(packed, mask):
    return jnp.where(mask, jnp.concatenate([packed] * (mask.shape[0] // packed.shape[0]), axis=0), 0.0)


def small_kernel(n, scale, root_ref, weight_ref, *refs):
    gathered = refs[:n]
    out, corr = refs[n], refs[n + 1]
    size = out.shape[0]
    root = root_ref[0]
    rows = lax.broadcasted_iota(jnp.int32, (size, size), 0)
    cols = lax.broadcasted_iota(jnp.int32, (size, size), 1)
    eye = (rows == cols).astype(jnp.float32)
    inv_lower = [gathered[j][:size, :size] for j in range(n)]
    known = {}

    def add(row, col, block):
        if row > col:
            row, col, block = col, row, block.T
        known[row, col] = block if (row, col) not in known else known[row, col] + block

    for s in range(0, n, CORES):
        for g in range(1, CORES):
            add(s ^ g, s, gathered[s][:size, g * size:(g + 1) * size])
    for s in range(n):
        chip, core = s // CORES, s % CORES
        column = 0
        for head in range(1, n // CORES):
            for other in range(head):
                for g in range(CORES):
                    block = gathered[s][size:, column * size:(column + 1) * size]
                    add(CORES * (other ^ chip) + (core ^ g), CORES * (head ^ chip) + core, block)
                    column += 1
    for j in range(n):
        corr[j, j] = eye
        for i in range(j + 1, n):
            block = mmt(mm(inv_lower[j], known[j, i]), inv_lower[i])
            corr[j, i] = block
            corr[i, j] = block.T
    middle = 2.0 / (1.0 + LOWEST)
    group = min(n, 4)
    wide = group * size
    mask = (
        lax.broadcasted_iota(jnp.int32, (wide, wide), 0) // size
        == lax.broadcasted_iota(jnp.int32, (wide, wide), 1) // size
    )
    eyes = jnp.concatenate([eye] * group, axis=1)
    lane = lax.broadcasted_iota(jnp.int32, (size, wide), 1) // size
    terms, phi = [], jnp.zeros((size, size), jnp.float32)

    def each(a, b):
        return mm(a, diagonal(b, mask))

    for first in range(0, n, group):
        m = [corr[root, first + g] for g in range(group)]
        k = jnp.concatenate([mmt(block, block) for block in m], axis=1)
        m = jnp.concatenate(m, axis=1)
        r = eyes - middle * k
        r2 = each(r, r)
        total = each(eyes + r, eyes + r2)
        r4 = each(r2, r2)
        total = each(total, eyes + r4)
        r8 = each(r4, r4)
        inv = middle * each(total, eyes + r8)
        inv = inv + each(inv, eyes - each(k, inv))
        right = each(inv, m)
        powers = {1: inv - eyes}
        for p in range(2, STEP + 1):
            powers[p] = each(powers[p // 2], powers[p - p // 2])
        factor = None
        for start in reversed(range(0, len(atan_coeffs), STEP)):
            block = atan_coeffs[start] * eyes
            for p in range(1, min(STEP, len(atan_coeffs) - start)):
                block = block + atan_coeffs[start + p] * powers[p]
            factor = block if factor is None else block + each(powers[STEP], factor)
        weight = jnp.zeros((size, wide), jnp.float32)
        for g in range(group):
            weight = jnp.where(lane == g, weight_ref[first + g], weight)
        factor = weight * factor
        term = each(factor, right)
        for g in range(group):
            phi = phi + factor[:, g * size:(g + 1) * size]
            terms.append(term[:, g * size:(g + 1) * size])
    energy = -mm(phi, phi)
    for j in range(n):
        column = terms[j].T
        for i in range(n):
            if i != j:
                column = column + mmt(corr[j, i], terms[i])
        energy = energy + mm(terms[j], column)
    right = []
    for j in range(n):
        right.append(mm(terms[j] - jnp.where(root == j, 1.0, 0.0) * phi, inv_lower[j]))
    lead = [jnp.where(root == j, 1.0, 0.0) * inv_lower[j] for j in range(n)]
    powers = powers_of(energy, STEP)
    both = [
        jnp.concatenate([jnp.full((1, size), c), jnp.full((1, size), s)], axis=1)
        for c, s in zip(cos_coeffs, sin_coeffs)
    ]
    twice = {p: jnp.concatenate([power] * 2, axis=1) for p, power in powers.items()}
    total = None
    for start in reversed(range(0, len(both), STEP)):
        block = both[start] * jnp.concatenate([eye] * 2, axis=1)
        for p in range(1, min(STEP, len(both) - start)):
            block = block + both[start + p] * twice[p]
        total = block if total is None else block + mm(powers[STEP], total)
    stacked = jnp.concatenate(
        [jnp.concatenate(lead, axis=1), jnp.concatenate(right, axis=1)], axis=0
    )
    out[...] = scale * mm(total, stacked)


def small(root, weights, gathered, size, scale):
    n = len(gathered)
    vmem = pl.BlockSpec(memory_space=pltpu.VMEM)
    smem = pl.BlockSpec(memory_space=pltpu.SMEM)
    return pl.pallas_call(
        functools.partial(small_kernel, n, scale),
        out_shape=jax.ShapeDtypeStruct((size, n * size), jnp.float32),
        in_specs=[smem, smem] + [vmem] * n,
        out_specs=vmem,
        scratch_shapes=[pltpu.VMEM((n, n, size, size), jnp.float32)],
        cost_estimate=pl.CostEstimate(
            flops=20000 * size**3, bytes_accessed=4 * 4 * n * size * size, transcendentals=0
        ),
        name="small",
    )(root, weights, *gathered)


def mix_kernel(n, where, coeffs, *refs):
    pieces, out = refs[:n], refs[-1]
    size = out.shape[0]
    high, middle, low = split(jnp.concatenate([piece[...] for piece in pieces], axis=0))
    left = jnp.concatenate(split(coeffs[...]), axis=0)
    first = jnp.dot(left, high, preferred_element_type=jnp.float32)
    second = jnp.dot(left[:2 * size], middle, preferred_element_type=jnp.float32)
    third = jnp.dot(left[:size], low, preferred_element_type=jnp.float32)
    small_part = first[2 * size:] + second[size:] + third
    out[...] = (small_part + (first[size:2 * size] + second[:size])) + first[:size]


def mix(place, coeffs, whole, parts, result, tile):
    size, cols = whole[0].shape
    part = parts[0].shape[1]
    tile = min(tile, part)
    steps = part // tile
    n = len(whole) + len(parts)
    at_place = pl.BlockSpec((size, tile), lambda i, w: (0, w[0] * steps + i))
    at_start = pl.BlockSpec((size, tile), lambda i, w: (0, i))
    specs = [pl.BlockSpec((size, n * size), lambda i, w: (0, 0))]
    specs += [at_place] * len(whole) + [at_start] * len(parts)
    operands = [place, coeffs, *whole, *parts]
    aliases = {}
    if result is not None:
        specs.append(pl.BlockSpec(memory_space=pl.ANY))
        aliases = {len(operands): 0}
        operands.append(result)
    return pl.pallas_call(
        functools.partial(mix_kernel, n),
        out_shape=jax.ShapeDtypeStruct((size, cols), jnp.float32),
        grid_spec=pltpu.PrefetchScalarGridSpec(
            num_scalar_prefetch=1, grid=(steps,), in_specs=specs, out_specs=at_place
        ),
        input_output_aliases=aliases,
        cost_estimate=pl.CostEstimate(
            flops=6 * 2 * n * size * size * part, bytes_accessed=4 * (n + 1) * size * part,
            transcendentals=0,
        ),
        name="mix",
    )(*operands)


def after(x, *deps):
    return lax.optimization_barrier((x, *deps))[0]


def counts(chips):
    return max(1, 4 // chips), max(1, 8 // chips)


def early_of(chips, far_count):
    return (chips - 1) ** 2 * far_count // 2


def on_device(snapshots, ref_index, weight_codes):
    own = snapshots[0]
    size, cols = own.shape
    n, mesh_size = lax.axis_size("variant"), lax.axis_size("mesh")
    chips = n // CORES
    part = cols // chips
    me = lax.axis_index("variant").astype(jnp.int32)
    chip = me // CORES
    near_count, far_count = counts(chips)
    early = early_of(chips, far_count)
    scale = math.sqrt(cols * mesh_size)
    codes = weight_codes.astype(jnp.float32)
    weights = (codes / jnp.sum(codes))[jnp.arange(n) ^ me]
    root = ref_index ^ me

    def move(x, offset):
        return lax.ppermute(x, "variant", xor_pairs(n, offset))

    def mesh_sum(x):
        step = 1
        while step < mesh_size:
            x = x + lax.ppermute(x, "mesh", xor_pairs(mesh_size, step))
            step *= 2
        return x

    def gather(x):
        both = jnp.concatenate([x, move(x, 1)], axis=0)
        blocks = [both]
        for offset in range(1, chips):
            blocks.append(move(both, CORES * offset))
        rows = x.shape[0]
        return [b[g * rows:(g + 1) * rows] for b in blocks for g in range(CORES)]

    def pieces_of(x, count, index, offset):
        chunk = part // count
        return lax.dynamic_slice(x, (0, (chip ^ offset) * part + index * chunk), (size, chunk))

    near, far = {}, {}
    source = own
    for c in range(near_count):
        for o in range(1, chips):
            piece = pieces_of(source, near_count, c, o)
            source = after(own, piece)
            near[o, c] = move(piece, CORES * o)
    partner = move(own, 1)
    for p in range(1, chips):
        for c in range(far_count):
            for o in range(1, chips):
                piece = pieces_of(source, far_count, c, o ^ p)
                far[o, p, c] = move(piece, CORES * o)
    zero = jnp.zeros((1,), jnp.int32)
    own_gram = gram(zero, [own], [own, partner], [], [CORES], None, cols, 4096)
    own_gram = mesh_sum(own_gram)
    lower = jnp.linalg.cholesky(own_gram[:, :size])
    inv_lower = jax.scipy.linalg.solve_triangular(lower, jnp.eye(size, dtype=jnp.float32), lower=True)
    ready = jnp.concatenate([inv_lower, own_gram[:, size:]], axis=1)

    cross = None
    others = {}
    for c in range(near_count):
        heads = [after(near[o, c], ready) for o in range(1, chips)]
        for o in range(1, chips):
            near[o, c] = heads[o - 1]
        columns = []
        for o in range(1, chips - 1):
            others[o, c] = move(near[o, c], 1)
            columns += [near[o, c], others[o, c]]
        cross = gram(
            (chip * near_count + c)[None], heads, [own, partner], columns,
            [CORES * o for o in range(1, chips)], cross, part // near_count, 2048,
        )
    cross = mesh_sum(cross)
    width = max(cross.shape[1], ready.shape[1])
    wide = lambda x: jnp.pad(x, ((0, 0), (0, width - x.shape[1])))
    gathered = gather(jnp.concatenate([wide(ready), wide(cross)], axis=0))
    coeffs = small(root, weights, gathered, size, scale)

    def forward(x, *deps):
        return move(after(x, *deps), 1)

    result = None
    for c in range(near_count):
        parts = []
        for o in range(1, chips):
            other = others[o, c] if (o, c) in others else forward(near[o, c], gathered[-1])
            parts += [near[o, c], other]
        result = mix((chip * near_count + c)[None], coeffs, [own, partner], parts, result, 2048)
    for p in range(1, chips):
        for c in range(far_count):
            parts = []
            for o in range(1, chips):
                number = (p - 1) * far_count * (chips - 1) + c * (chips - 1) + o - 1
                dep = gathered[-1] if number < early else coeffs
                parts += [far[o, p, c], forward(far[o, p, c], dep)]
            result = mix(((chip ^ p) * far_count + c)[None], coeffs, [own, partner], parts, result, 2048)
    return result


def solution(mesh):
    return jax.shard_map(
        on_device,
        mesh=mesh,
        in_specs=(P("variant", None, "mesh"), P(), P()),
        out_specs=P(None, "mesh"),
        check_vma=False,
    )
```

time: 382 us -> 173 us (0.45)
  blocking collectives: 113 us -> 0 us
  waiting for transfers between devices: 162 us -> 74.7 us
  matrix products: 64.9 us -> 0.23 us
  Pallas kernels: 0 us -> 49.6 us
  starting transfers between devices: 0.22 us -> 20.6 us
  between operations: 15.9 us -> 0.79 us
  local copies, waits for them, and re-layouts: 1.11 us -> 10.8 us
  other arithmetic: 24.8 us -> 15.4 us
    psum x2 -> x0, waiting for transfers between devices: 162 us -> none  [the longest x1 82.1 us: on_device(): blended = lax.psum(term, 'variant')]
    psum x3 -> x0, blocking collectives: 113 us -> none  [the longest x1 38.9 us: on_device(): gram_own = lax.psum(product(own_snap, own_snap.T), 'mesh')]
    ppermute x0 -> x21, waiting for transfers between devices: none -> 74.7 us  [the longest x15 63.9 us: move(): return lax.ppermute(x, 'variant', xor_pairs(n, offset))]
    dot_general x74 -> x0, matrix products: 55.2 us -> none  [product(): jnp.dot(left, right, precision=highest, preferred_element_type=jnp.float32)]
    pallas_call x0 -> x10, Pallas kernels: none -> 49.6 us  [the longest x6 20.6 us: mix(): pl.pallas_call(functools.partial(mix_kernel, n), out_shape=jax.ShapeDtype...]
    ppermute x0 -> x21, starting transfers between devices: none -> 20.6 us  [the longest x6 12 us: mesh_sum(): x = x + lax.ppermute(x, 'mesh', xor_pairs(mesh_size, step))]
    another operation x10 -> x5, other arithmetic: 24.2 us -> 12.2 us  [the longest x3 6.61 us: on_device(): lower = jnp.linalg.cholesky(own_gram[:, :size])]
    another operation x3 -> x1, matrix products: 9.69 us -> 0.23 us  [on_device(): jax.scipy.linalg.solve_triangular(lower, jnp.eye(size, dtype=jnp.float32)...]
  transfers between devices with their start and end apart: 2 -> 21, of which waited for: 2 -> 11; matrix products, arithmetic and copies ran while one was open for 0% -> 13% of each run, Pallas kernels for 0% -> 17%
where the time goes in v1:
time: 173 us; the launch traced here: 172 us
  waiting for transfers between devices  74.7 us (43%)
  Pallas kernels  49.6 us (29%)
  starting transfers between devices  20.6 us (12%)
  other arithmetic  15.4 us (9%)
  local copies, waits for them, and re-layouts  10.8 us (6%)
    ppermute x15, waiting for transfers between devices, move(): return lax.ppermute(x, 'variant', xor_pairs(n, offset))  63.9 us
    pallas_call x6, Pallas kernels, mix(): pl.pallas_call(functools.partial(mix_kernel, n), out_shape=jax.ShapeDtype...  20.6 us
    pallas_call x3, Pallas kernels, gram(): pl.pallas_call(functools.partial(gram_kernel, len(heads), groups, before...  17.9 us
    ppermute x6, starting transfers between devices, mesh_sum(): x = x + lax.ppermute(x, 'mesh', xor_pairs(mesh_size, step))  12 us
    pallas_call x1, Pallas kernels, small(): pl.pallas_call(functools.partial(small_kernel, n, scale), out_shape=jax.S...  11.1 us
    ppermute x6, waiting for transfers between devices, mesh_sum(): x = x + lax.ppermute(x, 'mesh', xor_pairs(mesh_size, step))  10.8 us
    ppermute x15, starting transfers between devices, move(): return lax.ppermute(x, 'variant', xor_pairs(n, offset))  8.58 us
    another operation x3, other arithmetic, on_device(): lower = jnp.linalg.cholesky(own_gram[:, :size])  6.61 us
  transfers between devices with their start and end apart: 21, of which 11 were waited for; matrix products, arithmetic and copies ran while one was open for 13% of the time, Pallas kernels for 17%

profile of v1, /device:TPU:0, one launch (start us, length us, event | category | flops | bytes accessed | tf_op | source)
XLA Modules:
  0.0 172.0 jit_solution(2729474020782440790)
XLA Ops:
  0.5 7.1 %collective-permute-done.refs_2_.refs_1_ = f32[64,16384]{1,0:T(8,128)} collective-permute-done((f32[64,16384]{1,0:T(8,128)}, f32[64,16384]{1,0:T(8,128)}, u32[]{:S(2)}, u32[]{:S(2)}) %collective-permute-start) | collective-permute-done | bytes 4194336 | tf_op jit(solution)/shard_map/ppermute | solution.py:324
  7.6 9.5 %shard_map.37 = f32[64,128]{1,0:T(8,128)} custom-call(s32[1]{0:T(128)} %constant.79.clone.1.where, f32[64,16384]{1,0:T(8,128)} %bitcast.23, f32[64,16384]{1,0:T(8,128)} %bitcast.24, f32[64,16384]{1,0:T(8,128)} %collective-permute-done.refs_2_.refs_1_), custom_call_target="tpu_custom_call" | custom-call | flops 2415919104 | bytes 12582912 | tf_op jit(solution)/shard_map/pallas_call | solution.py:108
  17.1 2.9 %collective-permute-start.1 = (f32[64,128]{1,0:T(8,128)}, f32[64,128]{1,0:T(8,128)S(1)}, u32[]{:S(2)}, u32[]{:S(2)}) collective-permute-start(f32[64,128]{1,0:T(8,128)} %shard_map.37), channel_id=1, source_target_pairs={{0,1},{1,0},{2,3},{3,2},{4,5},{5,4},{6,7},{7,6},{8,9},{9,8},{10,11... | collective-permute-start | bytes 98312 | tf_op jit(solution)/shard_map/ppermute | solution.py:329
  20.0 2.1 %collective-permute-done.1 = f32[64,128]{1,0:T(8,128)S(1)} collective-permute-done((f32[64,128]{1,0:T(8,128)}, f32[64,128]{1,0:T(8,128)S(1)}, u32[]{:S(2)}, u32[]{:S(2)}) %collective-permute-start.1) | collective-permute-done | bytes 32800 | tf_op jit(solution)/shard_map/ppermute | solution.py:329
  22.1 0.8 add.94
  22.8 2.1 %collective-permute-start.2 = (f32[64,128]{1,0:T(8,128)S(1)}, f32[64,128]{1,0:T(8,128)S(1)}, u32[]{:S(2)}, u32[]{:S(2)}) collective-permute-start(f32[64,128]{1,0:T(8,128)S(1)} %add.94), channel_id=1, source_target_pairs={{0,2},{1,3},{2,0},{3,1},{4,6},{5,7},{6,4},{7,5},{8,10},{9,11},{10,... | collective-permute-start | bytes 98312 | tf_op jit(solution)/shard_map/ppermute | solution.py:329
  24.9 1.3 dynamic-slice_bitcast_fusion
  26.2 1.6 collective-permute-start.5
  27.8 2.6 %collective-permute-start.3 = (f32[64,128]{1,0:T(8,128)S(1)}, f32[64,128]{1,0:T(8,128)S(1)}, u32[]{:S(2)}, u32[]{:S(2)}) collective-permute-start(f32[64,128]{1,0:T(8,128)S(1)} %add.95), channel_id=1, source_target_pairs={{0,4},{1,5},{2,6},{3,7},{4,0},{5,1},{6,2},{7,3},{8,12},{9,13},{10,... | collective-permute-start | bytes 98312 | tf_op jit(solution)/shard_map/ppermute | solution.py:329
  30.4 2.3 %constant_dynamic-slice_fusion.4 = f32[64,4096]{1,0:T(8,128)} fusion(f32[64,16384]{1,0:T(8,128)} %bitcast.25, s32[]{:T(128)S(6)} %select_n.41), kind=kLoop, calls=%fused_computation.21 | loop fusion | bytes 2097156 | tf_op jit(solution)/shard_map/dynamic_slice | solution.py:343
  32.7 0.9 collective-permute-start.4
  33.8 5.9 %cholesky.17 = f32[64,64]{1,0:T(8,128)S(1)} custom-call(f32[64,64]{1,0:T(8,128)S(1)} %get-tuple-element.31), custom_call_target="Cholesky" | custom-call | tf_op jit(solution)/shard_map/jit(cholesky)/cholesky | solution.py:361
  39.7 0.7 compare_reduce_fusion
  40.4 0.7 fusion
  41.1 4.9 %custom-call.7 = f32[1,64,64]{1,2,0:T(8,128)S(1)} custom-call(f32[1,64,64]{2,1,0:T(8,128)S(1)} %fusion), custom_call_target="InvertDiagBlocksLowerTriangular" | custom-call | tf_op jit(solution)/shard_map/jit(_solve_triangular)/triangular_solve | solution.py:362
  46.2 6.1 %collective-permute-done.5.refs_0_.refs_2_ = f32[64,4096]{1,0:T(8,128)S(1)} collective-permute-done((f32[64,4096]{1,0:T(8,128)S(1)}, f32[64,4096]{1,0:T(8,128)S(1)}, u32[]{:S(2)}, u32[]{:S(2)}) %collective-permute-start.5) | collective-permute-done | bytes 1048608 | tf_op jit(solution)/shard_map/ppermute | solution.py:324
  52.3 20.2 %collective-permute-done.4.refs_0_.refs_2_ = f32[64,4096]{1,0:T(8,128)S(1)} collective-permute-done((f32[64,4096]{1,0:T(8,128)}, f32[64,4096]{1,0:T(8,128)S(1)}, u32[]{:S(2)}, u32[]{:S(2)}) %collective-permute-start.4) | collective-permute-done | bytes 1048608 | tf_op jit(solution)/shard_map/ppermute | solution.py:324
  72.5 4.4 %shard_map.38.refs_3_ = f32[64,128]{1,0:T(8,128)} custom-call(s32[1]{0:T(128)} %bitcast.9.where, f32[64,4096]{1,0:T(8,128)} %copy-done, f32[64,16384]{1,0:T(8,128)} %bitcast.26, f32[64,16384]{1,0:T(8,128)} %collective-permute-done.refs_2_.refs_1_), custom_call_target="tpu_custom_call" | custom-call | flops 603979776 | bytes 3145728 | tf_op jit(solution)/shard_map/pallas_call | solution.py:108
  76.9 4.0 %shard_map.39 = f32[64,128]{1,0:T(8,128)} custom-call(s32[1]{0:T(128)} %bitcast.7.where, f32[64,4096]{1,0:T(8,128)} %copy-done.2, f32[64,16384]{1,0:T(8,128)} %bitcast.27, f32[64,16384]{1,0:T(8,128)} %collective-permute-done.refs_2_.refs_1_, f32[64,128]{1,0:T(8,128)} %shard_map.38.refs_3_), custom_call_target="tpu_custom_call" | custom-call | flops 603979776 | bytes 4194304 | tf_op jit(solution)/shard_map/pallas_call | solution.py:108
  80.9 1.6 collective-permute-start.6
  82.5 2.6 %collective-permute-done.6 = f32[64,128]{1,0:T(8,128)S(1)} collective-permute-done((f32[64,128]{1,0:T(8,128)}, f32[64,128]{1,0:T(8,128)S(1)}, u32[]{:S(2)}, u32[]{:S(2)}) %collective-permute-start.6) | collective-permute-done | bytes 32800 | tf_op jit(solution)/shard_map/ppermute | solution.py:329
  85.1 0.8 add.102
  86.2 3.7 %collective-permute-done.7 = f32[64,128]{1,0:T(8,128)S(1)} collective-permute-done((f32[64,128]{1,0:T(8,128)S(1)}, f32[64,128]{1,0:T(8,128)S(1)}, u32[]{:S(2)}, u32[]{:S(2)}) %collective-permute-start.7) | collective-permute-done | bytes 32800 | tf_op jit(solution)/shard_map/ppermute | solution.py:329
  89.9 2.5 %collective-permute-start.8 = (f32[64,128]{1,0:T(8,128)S(1)}, f32[64,128]{1,0:T(8,128)S(1)}, u32[]{:S(2)}, u32[]{:S(2)}) collective-permute-start(f32[64,128]{1,0:T(8,128)S(1)} %add.103), channel_id=1, source_target_pairs={{0,4},{1,5},{2,6},{3,7},{4,0},{5,1},{6,2},{7,3},{8,12},{9,13},{10,... | collective-permute-start | bytes 98312 | tf_op jit(solution)/shard_map/ppermute | solution.py:329
  92.4 2.3 %collective-permute-done.8 = f32[64,128]{1,0:T(8,128)S(1)} collective-permute-done((f32[64,128]{1,0:T(8,128)S(1)}, f32[64,128]{1,0:T(8,128)S(1)}, u32[]{:S(2)}, u32[]{:S(2)}) %collective-permute-start.8) | collective-permute-done | bytes 32800 | tf_op jit(solution)/shard_map/ppermute | solution.py:329
  94.9 1.2 collective-permute-done.9.refs_1_
  96.2 1.7 collective-permute-start.10
  97.9 2.7 %constant_dynamic-slice_fusion = (f32[64,2048]{1,0:T(8,128)S(1)}, f32[64,2048]{1,0:T(8,128)}, f32[64,2048]{1,0:T(8,128)}, f32[64,2048]{1,0:T(8,128)}) fusion(f32[64,16384]{1,0:T(8,128)} %bitcast.28, s32[]{:T(128)S(6)} %select_n.45, s32[]{:T(128)S(6)} %select_n.44, s32[]{:T(128)S(6)} %select_n.43, s32[]{:T(128)S(6)} %select_n.42), kind=kLoop, calls=%fused_computation.17 | loop fusion | bytes 4194320 | tf_op jit(solution)/shard_map/dynamic_slice | solution.py:343
  100.9 1.7 collective-permute-start.15
  102.9 0.7 fusion.5
  103.6 0.7 convert_reduce_fusion
  104.3 0.7 convert_divide_fusion
  105.0 0.6 collective-permute-start.19
  105.6 9.8 %collective-permute-done.17.refs_2_ = f32[64,2048]{1,0:T(8,128)S(1)} collective-permute-done((f32[64,2048]{1,0:T(8,128)S(1)}, f32[64,2048]{1,0:T(8,128)S(1)}, u32[]{:S(2)}, u32[]{:S(2)}) %collective-permute-start.17) | collective-permute-done | bytes 524320 | tf_op jit(solution)/shard_map/ppermute | solution.py:324
  115.4 0.8 copy-done.5
  117.2 1.2 gather_fusion
  118.4 8.3 %collective-permute-done.15.refs_2_ = f32[64,2048]{1,0:T(8,128)} collective-permute-done((f32[64,2048]{1,0:T(8,128)}, f32[64,2048]{1,0:T(8,128)}, u32[]{:S(2)}, u32[]{:S(2)}) %collective-permute-start.15) | collective-permute-done | bytes 524320 | tf_op jit(solution)/shard_map/ppermute | solution.py:324
  126.7 11.2 %collective-permute-done.13.refs_2_ = f32[64,2048]{1,0:T(8,128)} collective-permute-done((f32[64,2048]{1,0:T(8,128)}, f32[64,2048]{1,0:T(8,128)}, u32[]{:S(2)}, u32[]{:S(2)}) %collective-permute-start.13) | collective-permute-done | bytes 524320 | tf_op jit(solution)/shard_map/ppermute | solution.py:324
  137.9 11.1 %small.1.coeffs = f32[64,256]{1,0:T(8,128)} custom-call(s32[1]{0:T(128)S(6)} %xor.29.root_ref, f32[4]{0:T(128)} %gather_fusion, f32[128,128]{1,0:T(8,128)} %copy-done.7, f32[128,128]{1,0:T(8,128)} %copy-done.8, f32[128,128]{1,0:T(8,128)} %get-tuple-element.30.refs_2_, f32[128,128]{1,0:T(8,128)} %get-tuple-element.29.refs_3_), custom_call_target="tpu_custom_call" | custom-call | flops 5242880000 | bytes 262144 | tf_op jit(solution)/shard_map/small/pallas_call | solution.py:240
  149.0 0.5 collective-permute-start.14
  149.6 1.0 copy-done.4
  150.6 4.1 %mix.6.refs_4_ = f32[64,16384]{1,0:T(8,128)} custom-call(s32[1]{0:T(128)} %bitcast.9.where, f32[64,256]{1,0:T(8,128)} %small.1.coeffs, f32[64,16384]{1,0:T(8,128)} %bitcast.29, f32[64,16384]{1,0:T(8,128)} %collective-permute-done.refs_2_.refs_1_, f32[64,4096]{1,0:T(8,128)} %copy-done, f32[64,4096]{1,0:T(8,128)} %copy-done.4), custom_call_target="tpu_custom_call" | custom-call | flops 805306368 | bytes 5242880 | tf_op jit(solution)/shard_map/mix/pallas_call | solution.py:281
  154.7 4.1 %mix.7.refs_4_ = f32[64,16384]{1,0:T(8,128)} custom-call(s32[1]{0:T(128)} %bitcast.7.where, f32[64,256]{1,0:T(8,128)} %small.1.coeffs, f32[64,16384]{1,0:T(8,128)} %bitcast.30, f32[64,16384]{1,0:T(8,128)} %collective-permute-done.refs_2_.refs_1_, f32[64,4096]{1,0:T(8,128)} %copy-done.2, ...), custom_call_target="tpu_custom_call", output_to_operand_aliasing={{}: (6, {})} | custom-call | flops 805306368 | bytes 5242880 | tf_op jit(solution)/shard_map/mix/pallas_call | solution.py:281
  158.7 3.1 %mix.8.refs_4_ = f32[64,16384]{1,0:T(8,128)} custom-call(s32[1]{0:T(128)} %bitcast.12.where, f32[64,256]{1,0:T(8,128)} %small.1.coeffs, f32[64,16384]{1,0:T(8,128)} %bitcast.31, f32[64,16384]{1,0:T(8,128)} %collective-permute-done.refs_2_.refs_1_, f32[64,2048]{1,0:T(8,128)} %copy-done.5, ...), custom_call_target="tpu_custom_call", output_to_operand_aliasing={{}: (6, {})} | custom-call | flops 402653184 | bytes 2621440 | tf_op jit(solution)/shard_map/mix/pallas_call | solution.py:281
  161.9 3.1 %mix.9.refs_4_ = f32[64,16384]{1,0:T(8,128)} custom-call(s32[1]{0:T(128)} %bitcast.11.where, f32[64,256]{1,0:T(8,128)} %small.1.coeffs, f32[64,16384]{1,0:T(8,128)} %bitcast.32, f32[64,16384]{1,0:T(8,128)} %collective-permute-done.refs_2_.refs_1_, f32[64,2048]{1,0:T(8,128)} %collective-permute-done.15.refs_2_, ...), custom_call_target="tpu_custom_call", output_to_operand_aliasing={{}: (6, {})} | custom-call | flops 402653184 | bytes 2621440 | tf_op jit(solution)/shard_map/mix/pallas_call | solution.py:281
  165.0 3.1 %mix.10.refs_4_ = f32[64,16384]{1,0:T(8,128)} custom-call(s32[1]{0:T(128)} %bitcast.10.where, f32[64,256]{1,0:T(8,128)} %small.1.coeffs, f32[64,16384]{1,0:T(8,128)} %bitcast.33, f32[64,16384]{1,0:T(8,128)} %collective-permute-done.refs_2_.refs_1_, f32[64,2048]{1,0:T(8,128)} %collective-permute-done.13.refs_2_, ...), custom_call_target="tpu_custom_call", output_to_operand_aliasing={{}: (6, {})} | custom-call | flops 402653184 | bytes 2621440 | tf_op jit(solution)/shard_map/mix/pallas_call | solution.py:281
  168.1 0.8 copy-done.6
  168.9 3.1 %mix.11 = f32[64,16384]{1,0:T(8,128)} custom-call(s32[1]{0:T(128)} %bitcast.where, f32[64,256]{1,0:T(8,128)} %small.1.coeffs, f32[64,16384]{1,0:T(8,128)} %bitcast.34, f32[64,16384]{1,0:T(8,128)} %collective-permute-done.refs_2_.refs_1_, f32[64,2048]{1,0:T(8,128)} %collective-permute-done.11.refs_2_, ...), custom_call_target="tpu_custom_call", output_to_operand_aliasing={{}: (6, {})} | custom-call | flops 402653184 | bytes 2621440 | tf_op jit(solution)/shard_map/mix/pallas_call | solution.py:281
  (49 shorter events, 2.7 us)
Async XLA Ops:
  0.0 7.6 %collective-permute-start = (f32[64,16384]{1,0:T(8,128)}, f32[64,16384]{1,0:T(8,128)}, u32[]{:S(2)}, u32[]{:S(2)}) collective-permute-start(f32[64,16384]{1,0:T(8,128)} %bitcast.22), channel_id=1, source_target_pairs={{0,8},{8,0},{16,24},{24,16},{1,9},{9,1},{17,25},{25,17},{2,10},{10... | collective-permute-start | bytes 12582920 | tf_op jit(solution)/shard_map/ppermute | solution.py:324
  17.1 5.0 %collective-permute-start.1 = (f32[64,128]{1,0:T(8,128)}, f32[64,128]{1,0:T(8,128)S(1)}, u32[]{:S(2)}, u32[]{:S(2)}) collective-permute-start(f32[64,128]{1,0:T(8,128)} %shard_map.37), channel_id=1, source_target_pairs={{0,1},{1,0},{2,3},{3,2},{4,5},{5,4},{6,7},{7,6},{8,9},{9,8},{10,11... | collective-permute-start | bytes 98312 | tf_op jit(solution)/shard_map/ppermute | solution.py:329
  22.8 4.9 %collective-permute-start.2 = (f32[64,128]{1,0:T(8,128)S(1)}, f32[64,128]{1,0:T(8,128)S(1)}, u32[]{:S(2)}, u32[]{:S(2)}) collective-permute-start(f32[64,128]{1,0:T(8,128)S(1)} %add.94), channel_id=1, source_target_pairs={{0,2},{1,3},{2,0},{3,1},{4,6},{5,7},{6,4},{7,5},{8,10},{9,11},{10,... | collective-permute-start | bytes 98312 | tf_op jit(solution)/shard_map/ppermute | solution.py:329
  26.2 26.1 %collective-permute-start.5 = (f32[64,4096]{1,0:T(8,128)S(1)}, f32[64,4096]{1,0:T(8,128)S(1)}, u32[]{:S(2)}, u32[]{:S(2)}) collective-permute-start(f32[64,4096]{1,0:T(8,128)S(1)} %dynamic-slice_bitcast_fusion), channel_id=1, source_target_pairs={{0,16},{8,24},{16,0},{24,8},{1,17},{9,25},{17,1},{25,9},{2,18},{10... | collective-permute-start | bytes 3145736 | tf_op jit(solution)/shard_map/ppermute | solution.py:324
  27.8 5.8 %collective-permute-start.3 = (f32[64,128]{1,0:T(8,128)S(1)}, f32[64,128]{1,0:T(8,128)S(1)}, u32[]{:S(2)}, u32[]{:S(2)}) collective-permute-start(f32[64,128]{1,0:T(8,128)S(1)} %add.95), channel_id=1, source_target_pairs={{0,4},{1,5},{2,6},{3,7},{4,0},{5,1},{6,2},{7,3},{8,12},{9,13},{10,... | collective-permute-start | bytes 98312 | tf_op jit(solution)/shard_map/ppermute | solution.py:329
  32.7 39.8 %collective-permute-start.4 = (f32[64,4096]{1,0:T(8,128)}, f32[64,4096]{1,0:T(8,128)S(1)}, u32[]{:S(2)}, u32[]{:S(2)}) collective-permute-start(f32[64,4096]{1,0:T(8,128)} %constant_dynamic-slice_fusion.4), channel_id=1, source_target_pairs={{0,16},{8,24},{16,0},{24,8},{1,17},{9,25},{17,1},{25,9},{2,18},{10... | collective-permute-start | bytes 3145736 | tf_op jit(solution)/shard_map/ppermute | solution.py:324
  52.3 20.2 %copy-start = (f32[64,4096]{1,0:T(8,128)}, f32[64,4096]{1,0:T(8,128)S(1)}, u32[]{:S(2)}) copy-start(f32[64,4096]{1,0:T(8,128)S(1)} %collective-permute-done.5.refs_0_.refs_2_) | copy-start | bytes 3145732
  72.5 4.4 %copy-start.2 = (f32[64,4096]{1,0:T(8,128)}, f32[64,4096]{1,0:T(8,128)S(1)}, u32[]{:S(2)}) copy-start(f32[64,4096]{1,0:T(8,128)S(1)} %collective-permute-done.4.refs_0_.refs_2_) | copy-start | bytes 3145732
  80.9 22.7 %copy-start.1 = (f32[64,4096]{1,0:T(8,128)S(1)}, f32[64,4096]{1,0:T(8,128)}, u32[]{:S(2)}) copy-start(f32[64,4096]{1,0:T(8,128)} %copy-done) | copy-start | bytes 3145732
  80.9 22.7 %copy-start.9 = (s32[4]{0:T(128)S(1)}, s32[4]{0:T(128)}, u32[]{:S(2)}) copy-start(s32[4]{0:T(128)} %param.5) | copy-start | bytes 52
  80.9 24.1 %copy-start.3 = (f32[64,4096]{1,0:T(8,128)S(1)}, f32[64,4096]{1,0:T(8,128)}, u32[]{:S(2)}) copy-start(f32[64,4096]{1,0:T(8,128)} %copy-done.2) | copy-start | bytes 3145732
  80.9 4.2 %collective-permute-start.6 = (f32[64,128]{1,0:T(8,128)}, f32[64,128]{1,0:T(8,128)S(1)}, u32[]{:S(2)}, u32[]{:S(2)}) collective-permute-start(f32[64,128]{1,0:T(8,128)} %shard_map.39), channel_id=1, source_target_pairs={{0,1},{1,0},{2,3},{3,2},{4,5},{5,4},{6,7},{7,6},{8,9},{9,8},{10,11... | collective-permute-start | bytes 98312 | tf_op jit(solution)/shard_map/ppermute | solution.py:329
  85.9 4.0 %collective-permute-start.7 = (f32[64,128]{1,0:T(8,128)S(1)}, f32[64,128]{1,0:T(8,128)S(1)}, u32[]{:S(2)}, u32[]{:S(2)}) collective-permute-start(f32[64,128]{1,0:T(8,128)S(1)} %add.102), channel_id=1, source_target_pairs={{0,2},{1,3},{2,0},{3,1},{4,6},{5,7},{6,4},{7,5},{8,10},{9,11},{10,... | collective-permute-start | bytes 98312 | tf_op jit(solution)/shard_map/ppermute | solution.py:329
  89.9 4.8 %collective-permute-start.8 = (f32[64,128]{1,0:T(8,128)S(1)}, f32[64,128]{1,0:T(8,128)S(1)}, u32[]{:S(2)}, u32[]{:S(2)}) collective-permute-start(f32[64,128]{1,0:T(8,128)S(1)} %add.103), channel_id=1, source_target_pairs={{0,4},{1,5},{2,6},{3,7},{4,0},{5,1},{6,2},{7,3},{8,12},{9,13},{10,... | collective-permute-start | bytes 98312 | tf_op jit(solution)/shard_map/ppermute | solution.py:329
  94.8 43.1 %copy-start.7 = (f32[128,128]{1,0:T(8,128)}, f32[128,128]{1,0:T(8,128)S(1)}, u32[]{:S(2)}) copy-start(f32[128,128]{1,0:T(8,128)S(1)} %pad_maximum_fusion.1.refs_0_) | copy-start | bytes 196612
  94.8 1.3 collective-permute-start.9
  96.1 41.8 %copy-start.8 = (f32[128,128]{1,0:T(8,128)}, f32[128,128]{1,0:T(8,128)S(1)}, u32[]{:S(2)}) copy-start(f32[128,128]{1,0:T(8,128)S(1)} %collective-permute-done.9.refs_1_) | copy-start | bytes 196612
  96.2 6.7 %collective-permute-start.10 = (f32[256,128]{1,0:T(8,128)S(1)}, f32[256,128]{1,0:T(8,128)S(1)}, u32[]{:S(2)}, u32[]{:S(2)}) collective-permute-start(f32[256,128]{1,0:T(8,128)S(1)} %pad_maximum_fusion), channel_id=1, source_target_pairs={{0,16},{8,24},{16,0},{24,8},{1,17},{9,25},{17,1},{25,9},{2,18},{10... | collective-permute-start | bytes 393224 | tf_op jit(solution)/shard_map/ppermute | solution.py:324
  100.6 14.8 %collective-permute-start.17 = (f32[64,2048]{1,0:T(8,128)S(1)}, f32[64,2048]{1,0:T(8,128)S(1)}, u32[]{:S(2)}, u32[]{:S(2)}) collective-permute-start(f32[64,2048]{1,0:T(8,128)S(1)} %get-tuple-element.25), channel_id=1, source_target_pairs={{0,16},{8,24},{16,0},{24,8},{1,17},{9,25},{17,1},{25,9},{2,18},{10... | collective-permute-start | bytes 1572872 | tf_op jit(solution)/shard_map/ppermute | solution.py:324
  100.9 25.8 %collective-permute-start.15 = (f32[64,2048]{1,0:T(8,128)}, f32[64,2048]{1,0:T(8,128)}, u32[]{:S(2)}, u32[]{:S(2)}) collective-permute-start(f32[64,2048]{1,0:T(8,128)} %get-tuple-element.26), channel_id=1, source_target_pairs={{0,16},{8,24},{16,0},{24,8},{1,17},{9,25},{17,1},{25,9},{2,18},{10... | collective-permute-start | bytes 1572872 | tf_op jit(solution)/shard_map/ppermute | solution.py:324
  102.6 35.3 %collective-permute-start.13 = (f32[64,2048]{1,0:T(8,128)}, f32[64,2048]{1,0:T(8,128)}, u32[]{:S(2)}, u32[]{:S(2)}) collective-permute-start(f32[64,2048]{1,0:T(8,128)} %get-tuple-element.27), channel_id=1, source_target_pairs={{0,16},{8,24},{16,0},{24,8},{1,17},{9,25},{17,1},{25,9},{2,18},{10... | collective-permute-start | bytes 1572872 | tf_op jit(solution)/shard_map/ppermute | solution.py:324
  103.6 45.9 %collective-permute-start.20 = (f32[64,4096]{1,0:T(8,128)S(1)}, f32[64,4096]{1,0:T(8,128)S(1)}, u32[]{:S(2)}, u32[]{:S(2)}) collective-permute-start(f32[64,4096]{1,0:T(8,128)S(1)} %copy-done.1), channel_id=1, source_target_pairs={{0,8},{8,0},{16,24},{24,16},{1,9},{9,1},{17,25},{25,17},{2,10},{10... | collective-permute-start | bytes 3145736 | tf_op jit(solution)/shard_map/ppermute | solution.py:324
  105.0 49.6 %collective-permute-start.19 = (f32[64,4096]{1,0:T(8,128)S(1)}, f32[64,4096]{1,0:T(8,128)}, u32[]{:S(2)}, u32[]{:S(2)}) collective-permute-start(f32[64,4096]{1,0:T(8,128)S(1)} %copy-done.3), channel_id=1, source_target_pairs={{0,8},{8,0},{16,24},{24,16},{1,9},{9,1},{17,25},{25,17},{2,10},{10... | collective-permute-start | bytes 3145736 | tf_op jit(solution)/shard_map/ppermute | solution.py:324
  115.4 0.8 copy-start.5
  116.2 32.9 %collective-permute-start.11 = (f32[64,2048]{1,0:T(8,128)}, f32[64,2048]{1,0:T(8,128)}, u32[]{:S(2)}, u32[]{:S(2)}) collective-permute-start(f32[64,2048]{1,0:T(8,128)} %get-tuple-element.28), channel_id=1, source_target_pairs={{0,16},{8,24},{16,0},{24,8},{1,17},{9,25},{17,1},{25,9},{2,18},{10... | collective-permute-start | bytes 1572872 | tf_op jit(solution)/shard_map/ppermute | solution.py:324
  126.7 32.0 %collective-permute-start.18 = (f32[64,2048]{1,0:T(8,128)}, f32[64,2048]{1,0:T(8,128)}, u32[]{:S(2)}, u32[]{:S(2)}) collective-permute-start(f32[64,2048]{1,0:T(8,128)} %copy-done.5), channel_id=1, source_target_pairs={{0,8},{8,0},{16,24},{24,16},{1,9},{9,1},{17,25},{25,17},{2,10},{10... | collective-permute-start | bytes 1572872 | tf_op jit(solution)/shard_map/ppermute | solution.py:324
  137.9 23.9 %collective-permute-start.16 = (f32[64,2048]{1,0:T(8,128)}, f32[64,2048]{1,0:T(8,128)}, u32[]{:S(2)}, u32[]{:S(2)}) collective-permute-start(f32[64,2048]{1,0:T(8,128)} %collective-permute-done.15.refs_2_), channel_id=1, source_target_pairs={{0,8},{8,0},{16,24},{24,16},{1,9},{9,1},{17,25},{25,17},{2,10},{10... | collective-permute-start | bytes 1572872 | tf_op jit(solution)/shard_map/ppermute | solution.py:324
  149.0 16.0 %collective-permute-start.14 = (f32[64,2048]{1,0:T(8,128)}, f32[64,2048]{1,0:T(8,128)}, u32[]{:S(2)}, u32[]{:S(2)}) collective-permute-start(f32[64,2048]{1,0:T(8,128)} %collective-permute-done.13.refs_2_), channel_id=1, source_target_pairs={{0,8},{8,0},{16,24},{24,16},{1,9},{9,1},{17,25},{25,17},{2,10},{10... | collective-permute-start | bytes 1572872 | tf_op jit(solution)/shard_map/ppermute | solution.py:324
  149.5 1.1 copy-start.4
  149.5 18.6 %collective-permute-start.12 = (f32[64,2048]{1,0:T(8,128)}, f32[64,2048]{1,0:T(8,128)S(1)}, u32[]{:S(2)}, u32[]{:S(2)}) collective-permute-start(f32[64,2048]{1,0:T(8,128)} %collective-permute-done.11.refs_2_), channel_id=1, source_target_pairs={{0,8},{8,0},{16,24},{24,16},{1,9},{9,1},{17,25},{25,17},{2,10},{10... | collective-permute-start | bytes 1572872 | tf_op jit(solution)/shard_map/ppermute | solution.py:324
  168.1 0.8 copy-start.6

commit v2 on v0

v2 whole, which is shorter than its diff:
```python
import functools
import math

import jax
import jax.numpy as jnp
from jax import lax
from jax.experimental import pallas as pl
from jax.experimental.pallas import tpu as pltpu
from jax.sharding import PartitionSpec as P


highest = lax.Precision.HIGHEST
atan_coeffs = [(-1.0) ** k / (2 * k + 1) for k in range(24)]
cos_coeffs = [(-1.0) ** k / math.factorial(2 * k) for k in range(24)]
sin_coeffs = [(-1.0) ** k / math.factorial(2 * k + 1) for k in range(24)]

CORES = 2
LOWEST = 1.0 / 1.64
STEP = 6


def xor_pairs(size, offset):
    return [(i, i ^ offset) for i in range(size)]


def mm(a, b):
    return jnp.dot(a, b, precision=highest, preferred_element_type=jnp.float32)


def mmt(a, b):
    return lax.dot_general(
        a, b, (((1,), (1,)), ((), ())), precision=highest, preferred_element_type=jnp.float32
    )


def powers_of(matrix, top):
    powers = {1: matrix}
    for k in range(2, top + 1):
        powers[k] = mm(powers[k // 2], powers[k - k // 2])
    return powers


def split(x):
    high = x.astype(jnp.bfloat16)
    rest = x - high.astype(jnp.float32)
    middle = rest.astype(jnp.bfloat16)
    low = (rest - middle.astype(jnp.float32)).astype(jnp.bfloat16)
    return high, middle, low


def raw_gram(a, b):
    return lax.dot_general(a, b, (((1,), (1,)), ((), ())), preferred_element_type=jnp.float32)


def raw_product(a, b):
    return jnp.dot(a, b, preferred_element_type=jnp.float32)


def fold(total, rows):
    tall = total.shape[0] // 3
    part = lambda i, j: total[i * tall:(i + 1) * tall, j * rows:(j + 1) * rows]
    order = sorted(((i, j) for i in range(3) for j in range(3)), key=lambda ij: -sum(ij))
    result = part(*order[0])
    for ij in order[1:]:
        result = result + part(*ij)
    return result


def load(refs, starts, slots, sems, tile):
    steps = slots[0].shape[1] // tile
    waits = []
    for t in range(steps):
        copies = []
        for index, (ref, start, slot) in enumerate(zip(refs, starts, slots)):
            first = start + t * tile
            if not isinstance(first, int):
                first = pl.multiple_of(first, 128)
            copies.append(
                pltpu.make_async_copy(
                    ref.at[:, pl.ds(first, tile)], slot.at[:, pl.ds(t * tile, tile)], sems.at[index, t]
                )
            )
            copies[-1].start()
        waits.append(copies)
    return waits


def gram_kernel(heads, groups, prior, at, whole, tile, where, *refs):
    count = (len(refs) - 2 - (1 if prior else 0)) // 2
    loaded, out = refs[:count], refs[count + (1 if prior else 0)]
    slots, sems = refs[-1 - count:-1], refs[-1]
    size, extent = slots[0].shape
    start = at(where) * extent
    waits = load(loaded, [start] * whole + [0] * (count - whole), slots, sems, tile)
    totals = [None] * len(heads)
    for t, copies in enumerate(waits):
        for copy in copies:
            copy.wait()
        pieces = [split(slot[:, t * tile:(t + 1) * tile]) for slot in slots]
        for index, (head, columns) in enumerate(zip(heads, groups)):
            right = jnp.concatenate(pieces[head], axis=0)
            left = jnp.concatenate([pieces[g][level] for level in range(3) for g in columns], axis=0)
            value = raw_gram(left, right)
            totals[index] = value if totals[index] is None else totals[index] + value
    blocks = []
    for columns, total in zip(groups, totals):
        result = fold(total, size)
        blocks += [result[g * size:(g + 1) * size] for g in range(len(columns))]
    result = jnp.concatenate(blocks, axis=1)
    out[...] = result + refs[count][...] if prior else result


def gram(where, at, whole, parts, heads, groups, before, extent, tile):
    size = (whole + parts)[0].shape[0]
    tile = min(tile, extent)
    width = sum(len(columns) for columns in groups) * size
    operands = [*whole, *parts]
    count = len(operands)
    vmem = pl.BlockSpec(memory_space=pltpu.VMEM)
    specs = [pl.BlockSpec(memory_space=pltpu.SMEM)] + [pl.BlockSpec(memory_space=pl.ANY)] * count
    if before is not None:
        operands.append(before)
        specs.append(vmem)
    return pl.pallas_call(
        functools.partial(gram_kernel, heads, groups, before is not None, at, len(whole), tile),
        out_shape=jax.ShapeDtypeStruct((size, width), jnp.float32),
        in_specs=specs,
        out_specs=vmem,
        scratch_shapes=[pltpu.VMEM((size, extent), jnp.float32)] * count
        + [pltpu.SemaphoreType.DMA((count, extent // tile))],
        cost_estimate=pl.CostEstimate(
            flops=9 * 2 * size * width * extent, transcendentals=0,
            bytes_accessed=4 * count * size * extent,
        ),
    )(where, *operands)


def invert_kernel(ref, out):
    size = ref.shape[0]
    rows = lax.broadcasted_iota(jnp.int32, (size, size), 0)
    cols = lax.broadcasted_iota(jnp.int32, (size, size), 1)
    eye = (rows == cols).astype(jnp.float32)
    index = lax.broadcasted_iota(jnp.int32, (size, 1), 0)
    work = jnp.concatenate([ref[:, :size], eye], axis=1)
    for j in range(size - 1):
        row = work[j:j + 1, :]
        factor = jnp.where(index > j, work[:, j:j + 1] / row[:, j:j + 1], 0.0)
        work = work - factor * row
    pivots = jnp.sum(work[:, :size] * eye, axis=1, keepdims=True)
    out[:, :size] = work[:, size:] / jnp.sqrt(pivots)
    out[:, size:] = ref[:, size:]


def invert(matrix):
    vmem = pl.BlockSpec(memory_space=pltpu.VMEM)
    return pl.pallas_call(
        invert_kernel,
        out_shape=jax.ShapeDtypeStruct(matrix.shape, jnp.float32),
        in_specs=[vmem],
        out_specs=vmem,
        cost_estimate=pl.CostEstimate(
            flops=4000 * matrix.shape[0] ** 2, bytes_accessed=8 * matrix.size, transcendentals=0
        ),
        name="invert",
    )(matrix)


def diagonal(packed, mask):
    return jnp.where(mask, jnp.concatenate([packed] * (mask.shape[0] // packed.shape[0]), axis=0), jnp.zeros((), packed.dtype))


def small_kernel(n, scale, me_ref, root_ref, code_ref, *refs):
    chips = n // CORES
    gathered, (out, gram_ref, corr) = refs[:chips], refs[chips:]
    size = out.shape[0]
    rows = gathered[0].shape[0] // CORES
    me = me_ref[0]
    root = root_ref[0] ^ me
    codes = [code_ref[j ^ me] for j in range(n)]
    eye = (
        lax.broadcasted_iota(jnp.int32, (size, size), 0)
        == lax.broadcasted_iota(jnp.int32, (size, size), 1)
    ).astype(jnp.float32)
    known = {}

    def add(row, col, block):
        if row > col:
            row, col, block = col, row, block.T
        known[row, col] = block if (row, col) not in known else known[row, col] + block

    lowers = []
    for s in range(n):
        chip, core = s // CORES, s % CORES
        ref, top = gathered[chip], core * rows
        lowers.append(ref[top:top + size, :size])
        add(s ^ 1, s, ref[top:top + size, size:CORES * size])
        column = 0
        for head in range(1, chips):
            for other in range(head):
                for g in range(CORES):
                    block = ref[top + size:top + 2 * size, column * size:(column + 1) * size]
                    add(CORES * (other ^ chip) + (core ^ g), CORES * (head ^ chip) + core, block)
                    column += 1
    zero = jnp.zeros((size, size), jnp.float32)
    for j in range(n):
        line = [zero if i == j else known[j, i] if j < i else known[i, j].T for i in range(n)]
        gram_ref[j * size:(j + 1) * size, :] = jnp.concatenate(line, axis=1)

    def block_mask(count):
        shape = (count * size, count * size)
        return (
            lax.broadcasted_iota(jnp.int32, shape, 0) // size
            == lax.broadcasted_iota(jnp.int32, shape, 1) // size
        )

    group = CORES
    wide = group * size
    every, mask = block_mask(n), block_mask(group)
    lower = jnp.concatenate(lowers, axis=1)
    spread = diagonal(lower, every)
    shape = (n * size, n * size)
    whole_eye = (
        lax.broadcasted_iota(jnp.int32, shape, 0) == lax.broadcasted_iota(jnp.int32, shape, 1)
    ).astype(jnp.float32)
    corr[...] = jnp.where(every, whole_eye, mmt(mm(spread, gram_ref[...]), spread))
    to_root = corr[pl.ds(pl.multiple_of(root * size, size), size), :]

    middle = 2.0 / (1.0 + LOWEST)
    eyes = jnp.concatenate([eye] * group, axis=1)
    lane = lax.broadcasted_iota(jnp.int32, (1, wide), 1) // size

    def each(a, b, product=raw_product):
        high, middle, low = [diagonal(x, mask) for x in split(b)]
        left = jnp.concatenate(split(a), axis=0)
        one = product(left, jnp.concatenate([high, middle], axis=product is raw_product))
        two = product(left[:size], low)
        little = one[2 * size:, :wide] + one[size:2 * size, wide:] + two
        return (little + (one[size:2 * size, :wide] + one[:size, wide:])) + one[:size, :wide]

    def groups(x):
        return [x[:, first * size:first * size + wide] for first in range(0, n, group)]

    terms, phi = [], zero
    for number, m in enumerate(groups(to_root)):
        k = each(m, m, raw_gram)
        r = eyes - middle * k
        r2 = each(r, r)
        total = each(eyes + r, eyes + r2)
        r4 = each(r2, r2)
        total = each(total, eyes + r4)
        r8 = each(r4, r4)
        inv = middle * each(total, eyes + r8)
        right = each(inv, m)
        powers = {1: inv - eyes}
        for p in range(2, STEP + 1):
            powers[p] = each(powers[p // 2], powers[p - p // 2])
        factor = None
        for start in reversed(range(0, len(atan_coeffs), STEP)):
            block = atan_coeffs[start] * eyes
            for p in range(1, min(STEP, len(atan_coeffs) - start)):
                block = block + atan_coeffs[start + p] * powers[p]
            factor = block if factor is None else block + each(powers[STEP], factor)
        weight = jnp.zeros((1, wide), jnp.int32)
        for g in range(group):
            weight = jnp.where(lane == g, codes[number * group + g], weight)
        all_codes = jnp.full((1, wide), sum(codes), jnp.int32)
        factor = (weight.astype(jnp.float32) / all_codes.astype(jnp.float32)) * factor
        for g in range(group):
            phi = phi + factor[:, g * size:(g + 1) * size]
        terms.append(each(factor, right))
    term = jnp.concatenate(terms, axis=1)
    energy = mmt(mm(term, corr[...]), term) - mm(phi, phi)
    at_root = lax.broadcasted_iota(jnp.int32, (1, n * size), 1) // size == root
    term = term - jnp.where(at_root, jnp.concatenate([phi] * n, axis=1), 0.0)
    right = [each(a, b) for a, b in zip(groups(term), groups(lower))]
    stacked = jnp.concatenate(
        [jnp.where(at_root, lower, 0.0), jnp.concatenate(right, axis=1)], axis=0
    )
    powers = powers_of(energy, STEP)
    both = [
        jnp.concatenate([jnp.full((1, size), c), jnp.full((1, size), s)], axis=1)
        for c, s in zip(cos_coeffs, sin_coeffs)
    ]
    twice = {p: jnp.concatenate([power] * 2, axis=1) for p, power in powers.items()}
    total = None
    for start in reversed(range(0, len(both), STEP)):
        block = both[start] * jnp.concatenate([eye] * 2, axis=1)
        for p in range(1, min(STEP, len(both) - start)):
            block = block + both[start + p] * twice[p]
        total = block if total is None else block + mm(powers[STEP], total)
    out[...] = scale * mm(total, stacked)


def small(me, root, codes, gathered, size, scale):
    n = len(gathered) * CORES
    vmem = pl.BlockSpec(memory_space=pltpu.VMEM)
    smem = pl.BlockSpec(memory_space=pltpu.SMEM)
    return pl.pallas_call(
        functools.partial(small_kernel, n, scale),
        out_shape=jax.ShapeDtypeStruct((size, n * size), jnp.float32),
        in_specs=[smem, smem, smem] + [vmem] * len(gathered),
        out_specs=vmem,
        scratch_shapes=[pltpu.VMEM((n * size, n * size), jnp.float32)] * 2,
        cost_estimate=pl.CostEstimate(
            flops=20000 * size**3, bytes_accessed=4 * 4 * n * size * size, transcendentals=0
        ),
        name="small",
    )(me, root, codes, *gathered)


def mix_kernel(whole, chunks, tile, aliased, where, coeffs, *refs):
    loaded = refs[:whole + sum(count for _, count, _ in chunks)]
    slots = refs[-3 - whole - chunks[0][1]:-3]
    out, (sums, in_sems, out_sems) = refs[len(loaded) + aliased], refs[-3:]
    size = sums.shape[0]
    waits, places, begun = [], [], whole
    for at, count, width in chunks:
        group = loaded[:whole] + loaded[begun:begun + count]
        begun += count
        for t in range(width // tile):
            number, copies = len(waits), []
            place = pl.ds(pl.multiple_of(at(where) + t * tile, 128), tile)
            for index, (ref, slot) in enumerate(zip(group, slots)):
                copies.append(
                    pltpu.make_async_copy(
                        ref.at[:, place if index < whole else pl.ds(t * tile, tile)],
                        slot.at[:, pl.ds(number * tile, tile)],
                        in_sems.at[index, number],
                    )
                )
                copies[-1].start()
            waits.append(copies)
            places.append(place)
    left = jnp.concatenate(split(coeffs[...]), axis=0)
    stores = []
    for t, copies in enumerate(waits):
        for copy in copies:
            copy.wait()
        here = slice(t * tile, (t + 1) * tile)
        high, middle, low = split(jnp.concatenate([slot[:, here] for slot in slots], axis=0))
        one = jnp.dot(left, high, preferred_element_type=jnp.float32)
        two = jnp.dot(left[:2 * size], middle, preferred_element_type=jnp.float32)
        three = jnp.dot(left[:size], low, preferred_element_type=jnp.float32)
        little = one[2 * size:] + two[size:] + three
        sums[:, here] = (little + (one[size:2 * size] + two[:size])) + one[:size]
        stores.append(
            pltpu.make_async_copy(
                sums.at[:, pl.ds(t * tile, tile)],
                out.at[:, places[t]],
                out_sems.at[t],
            )
        )
        stores[-1].start()
    for store in stores:
        store.wait()


def mix(where, coeffs, whole, chunks, result, tile):
    size, cols = whole[0].shape
    n = len(whole) + len(chunks[0][1])
    layout, extent, operands = [], 0, []
    for at, parts in chunks:
        layout.append((at, len(parts), parts[0].shape[1]))
        extent += parts[0].shape[1]
        operands += parts
    hbm = pl.BlockSpec(memory_space=pl.ANY)
    vmem = pl.BlockSpec(memory_space=pltpu.VMEM)
    operands = [where, coeffs, *whole, *operands]
    aliases = {}
    if result is not None:
        aliases = {len(operands): 0}
        operands.append(result)
    specs = [pl.BlockSpec(memory_space=pltpu.SMEM), vmem] + [hbm] * (len(operands) - 2)
    return pl.pallas_call(
        functools.partial(mix_kernel, len(whole), layout, tile, len(aliases)),
        out_shape=jax.ShapeDtypeStruct((size, cols), jnp.float32),
        in_specs=specs,
        out_specs=hbm,
        scratch_shapes=[pltpu.VMEM((size, extent), jnp.float32)] * (n + 1)
        + [pltpu.SemaphoreType.DMA((n, extent // tile)), pltpu.SemaphoreType.DMA((extent // tile,))],
        input_output_aliases=aliases,
        cost_estimate=pl.CostEstimate(
            flops=6 * 2 * n * size * size * extent, transcendentals=0,
            bytes_accessed=4 * (n + 1) * size * extent,
        ),
        name="mix",
    )(*operands)


def after(x, *deps):
    return lax.optimization_barrier((x, *deps))[0]


def widths(chips):
    return ((8, 4, 4), (8, 4, 4)) if chips == 2 else ((16,), (8, 8))


def early_of(chips):
    return 1 if chips == 2 else (chips - 1) ** 2


def starts_of(parts):
    return [sum(parts[:c]) for c in range(len(parts))]


def far_names(chips):
    others = range(1, chips)
    return [(o, p, c) for p in others for c in range(len(widths(chips)[1])) for o in others]


def on_device(snapshots, ref_index, weight_codes):
    own = snapshots[0]
    size, cols = own.shape
    n, mesh_size = lax.axis_size("variant"), lax.axis_size("mesh")
    chips = n // CORES
    part = cols // chips
    unit = part // 16
    me = lax.axis_index("variant").astype(jnp.int32)
    chip = me // CORES
    near_widths, far_widths = widths(chips)
    early = far_names(chips)[:early_of(chips)]
    scale = math.sqrt(cols * mesh_size)

    def move(x, offset):
        return lax.ppermute(x, "variant", xor_pairs(n, offset))

    def forward(x, *deps):
        return move(after(x, *deps), 1)

    def mesh_sum(x, beside=()):
        step, beside = 1, list(beside)
        while step < mesh_size:
            arrived = lax.ppermute(x, "mesh", xor_pairs(mesh_size, step))
            done = [beside.pop(0)(x)] if beside else []
            x = x + after(arrived, *done)
            step *= 2
        for call in beside:
            call(x)
        return x

    def gather(x):
        other = move(x, 1)
        both = jnp.concatenate([x, other], axis=0)
        blocks = [both]
        for offset in range(1, chips):
            blocks.append(move(both, CORES * offset))
        return blocks

    def piece_of(x, offset, start, width):
        return lax.dynamic_slice(
            x, (0, (chip ^ offset) * part + start * unit), (size, width * unit)
        )

    near, far = {}, {}
    where = me[None]
    near_starts, far_starts = starts_of(near_widths), starts_of(far_widths)
    for o in range(1, chips):
        near[o, 0] = move(piece_of(own, o, 0, near_widths[0]), CORES * o)
    partner = move(own, 1)
    own_gram = mmt(own, own)

    def send_near(c, source):
        for o in range(1, chips):
            piece = piece_of(source, o, near_starts[c], near_widths[c])
            near[o, c] = move(piece, CORES * o)
        return piece

    def send_far(o, p, c, source):
        piece = piece_of(source, o ^ p, far_starts[c], far_widths[c])
        far[o, p, c] = move(piece, CORES * o)
        return piece

    pair_gram = gram(
        where, lambda w: w[0] % CORES, [own, partner], [], [0], [(1,)], None, cols // CORES, 2048
    )
    calls = [lambda x, c=c: send_near(c, after(own, x)) for c in range(1, len(near_widths))]
    calls += [lambda x, key=key: send_far(*key, after(own, x)) for key in early]
    own_gram = mesh_sum(jnp.concatenate([own_gram, pair_gram], axis=1), calls)

    cross, others = None, {}
    ready = invert(own_gram) if len(near_widths) == 1 else own_gram
    for c, (start, width) in enumerate(zip(near_starts, near_widths)):
        dep = ready if cross is None else cross
        heads = [after(near[o, c], dep) for o in range(1, chips)]
        if c == 1:
            ready = invert(after(own_gram, cross))
            cross = after(cross, ready)
        columns, groups = [], [tuple(range(CORES))]
        for o in range(1, chips):
            near[o, c] = heads[o - 1]
        for o in range(1, chips - 1):
            others[o, c] = move(near[o, c], 1)
            columns.append(others[o, c])
        heads_at = [CORES + o for o in range(chips - 1)]
        for o in range(1, chips - 1):
            groups.append(groups[-1] + (heads_at[o - 1], CORES + chips - 1 + o - 1))
        cross = gram(
            where, lambda w, start=start, width=width: (w[0] // CORES * 16 + start) // width,
            [own, partner], heads + columns, heads_at, groups, cross, width * unit, 1024,
        )
    late = [key for key in far_names(chips) if key not in early]
    cross = mesh_sum(cross, [lambda x, key=key: send_far(*key, after(own, x)) for key in late])
    width = max(cross.shape[1], ready.shape[1])
    wide = lambda x: jnp.pad(x, ((0, 0), (0, width - x.shape[1])))
    gathered = gather(jnp.concatenate([wide(ready), wide(cross)], axis=0))
    coeffs = small(me[None], ref_index, weight_codes, gathered, size, scale)

    def at_near(start):
        return lambda w: w[0] // CORES * part + start * unit

    def at_far(p, start):
        return lambda w: (w[0] // CORES ^ p) * part + start * unit

    def far_parts(p, c, dep):
        parts = []
        for o in range(1, chips):
            parts += [far[o, p, c], forward(far[o, p, c], dep)]
        return at_far(p, far_starts[c]), parts

    chunks = []
    for c in range(len(near_widths)):
        parts = []
        for o in range(1, chips):
            other = others[o, c] if (o, c) in others else forward(near[o, c], cross)
            parts += [near[o, c], other]
        chunks.append((at_near(near_starts[c]), parts))
    places = [(p, c) for p in range(1, chips) for c in range(len(far_widths))]
    first = [(p, c) for p, c in places if all((o, p, c) in early for o in range(1, chips))]
    chunks += [far_parts(p, c, cross) for p, c in first]
    result = mix(where, coeffs, [own, partner], chunks, None, 2 * unit)
    results = [coeffs, result]
    for p, c in places:
        if (p, c) not in first:
            chunk = far_parts(p, c, results[-2])
            result = mix(where, coeffs, [own, partner], [chunk], result, 2 * unit)
            results.append(result)
    return result


def solution(mesh):
    return jax.shard_map(
        on_device,
        mesh=mesh,
        in_specs=(P("variant", None, "mesh"), P(), P()),
        out_specs=P(None, "mesh"),
        check_vma=False,
    )
```

time: 382 us -> 124 us (0.32)
  waiting for transfers between devices: 162 us -> 22.9 us
  blocking collectives: 113 us -> 0 us
  matrix products: 64.9 us -> 6.94 us
  Pallas kernels: 0 us -> 47.9 us
  starting transfers between devices: 0.22 us -> 24.4 us
  other arithmetic: 24.8 us -> 3.08 us
  local copies, waits for them, and re-layouts: 1.11 us -> 16.9 us
  between operations: 15.9 us -> 1.02 us
    psum x2 -> x0, waiting for transfers between devices: 162 us -> none  [the longest x1 82.1 us: on_device(): blended = lax.psum(term, 'variant')]
    psum x3 -> x0, blocking collectives: 113 us -> none  [the longest x1 38.9 us: on_device(): gram_own = lax.psum(product(own_snap, own_snap.T), 'mesh')]
    dot_general x74 -> x1, matrix products: 55.2 us -> 6.94 us  [mmt(): lax.dot_general(a, b, (((1,), (1,)), ((), ())), precision=highest, prefer...]
    pallas_call x0 -> x9, Pallas kernels: none -> 47.9 us  [the longest x3 15.8 us: mix(): pl.pallas_call(functools.partial(mix_kernel, len(whole), layout, tile, le...]
    ppermute x0 -> x21, starting transfers between devices: none -> 24.4 us  [the longest x6 12.9 us: mesh_sum(): arrived = lax.ppermute(x, 'mesh', xor_pairs(mesh_size, step))]
    another operation x10 -> x0, other arithmetic: 24.2 us -> none  [the longest x3 6.52 us: on_device(): lower_own = jnp.linalg.cholesky(gram_own)]
    ppermute x0 -> x21, waiting for transfers between devices: none -> 22.9 us  [the longest x15 17.8 us: move(): return lax.ppermute(x, 'variant', xor_pairs(n, offset))]
    dynamic_slice x1 -> x6, local copies, waits for them, and re-layouts: 0.56 us -> 11.3 us  [piece_of(): lax.dynamic_slice(x, (0, (chip ^ offset) * part + start * unit), (size, w...]
  transfers between devices with their start and end apart: 2 -> 21, of which waited for: 2 -> 7; matrix products, arithmetic and copies ran while one was open for 0% -> 17% of each run, Pallas kernels for 0% -> 36%
where the time goes in v2:
time: 124 us; the launch traced here: 123 us
  Pallas kernels  47.9 us (39%)
  starting transfers between devices  24.4 us (20%)
  waiting for transfers between devices  22.9 us (18%)
  local copies, waits for them, and re-layouts  16.9 us (14%)
  matrix products  6.94 us (6%)
  other arithmetic  3.08 us (2%)
    ppermute x15, waiting for transfers between devices, move(): return lax.ppermute(x, 'variant', xor_pairs(n, offset))  17.8 us
    pallas_call x3, Pallas kernels, mix(): pl.pallas_call(functools.partial(mix_kernel, len(whole), layout, tile, le...  15.8 us
    pallas_call x4, Pallas kernels, gram(): pl.pallas_call(functools.partial(gram_kernel, heads, groups, before is no...  15.5 us
    ppermute x6, starting transfers between devices, mesh_sum(): arrived = lax.ppermute(x, 'mesh', xor_pairs(mesh_size, step))  12.9 us
    ppermute x15, starting transfers between devices, move(): return lax.ppermute(x, 'variant', xor_pairs(n, offset))  11.5 us
    dynamic_slice x6, local copies, waits for them, and re-layouts, piece_of(): lax.dynamic_slice(x, (0, (chip ^ offset) * part + start * unit), (size, w...  11.3 us
    pallas_call x1, Pallas kernels, small(): pl.pallas_call(functools.partial(small_kernel, n, scale), out_shape=jax.S...  9.79 us
    dot_general x1, matrix products, mmt(): lax.dot_general(a, b, (((1,), (1,)), ((), ())), precision=highest, prefer...  6.94 us
  transfers between devices with their start and end apart: 21, of which 7 were waited for; matrix products, arithmetic and copies ran while one was open for 17% of the time, Pallas kernels for 36%

profile of v2, /device:TPU:0, one launch (start us, length us, event | category | flops | bytes accessed | tf_op | source)
XLA Modules:
  0.0 123.1 jit_solution(14017876098310986101)
XLA Ops:
  0.0 0.5 collective-permute-start
  0.5 2.3 %dynamic-slice_bitcast_fusion = f32[64,4096]{1,0:T(8,128)} fusion(f32[1,64,16384]{2,1,0:T(8,128)} %param.3, s32[]{:T(128)S(6)} %select_n.27), kind=kLoop, calls=%fused_computation | loop fusion | bytes 2097156 | tf_op jit(solution)/shard_map/dynamic_slice | solution.py:450
  2.8 2.5 %collective-permute-start.4 = (f32[64,4096]{1,0:T(8,128)}, f32[64,4096]{1,0:T(8,128)S(1)}, u32[]{:S(2)}, u32[]{:S(2)}) collective-permute-start(f32[64,4096]{1,0:T(8,128)} %dynamic-slice_bitcast_fusion), channel_id=1, source_target_pairs={{0,16},{8,24},{16,0},{24,8},{1,17},{9,25},{17,1},{25,9},{2,18},{10... | collective-permute-start | bytes 3145736 | tf_op jit(solution)/shard_map/ppermute | solution.py:425
  5.2 6.9 %fusion = f32[64,64]{1,0:T(8,128)S(1)} fusion(f32[1,64,16384]{2,1,0:T(8,128)} %param.3), kind=kOutput, calls=%fused_computation.9 | convolution fusion | flops 805306368 | bytes 4210688 | tf_op jit(solution)/shard_map/dot_general | solution.py:31
  12.2 4.3 %shard_map.37 = f32[64,64]{1,0:T(8,128)} custom-call(s32[1]{0:T(128)} %bitcast.where.me_ref, f32[64,16384]{1,0:T(8,128)} %bitcast.7, f32[64,16384]{1,0:T(8,128)} %collective-permute-done.refs_1_), custom_call_target="tpu_custom_call" | custom-call | flops 603979776 | bytes 4194304 | tf_op jit(solution)/shard_map/pallas_call | solution.py:124
  16.5 0.8 pad_maximum_fusion.2
  17.3 1.5 %collective-permute-start.1 = (f32[64,128]{1,0:T(8,128)S(1)}, f32[64,128]{1,0:T(8,128)S(1)}, u32[]{:S(2)}, u32[]{:S(2)}) collective-permute-start(f32[64,128]{1,0:T(8,128)S(1)} %pad_maximum_fusion.2), channel_id=1, source_target_pairs={{0,1},{1,0},{2,3},{3,2},{4,5},{5,4},{6,7},{7,6},{8,9},{9,8},{10,11... | collective-permute-start | bytes 98312 | tf_op jit(solution)/shard_map/ppermute | solution.py:433
  18.8 1.9 %constant_dynamic-slice_fusion.4 = f32[64,2048]{1,0:T(8,128)} fusion(f32[64,16384]{1,0:T(8,128)} %bitcast.8, s32[]{:T(128)S(6)} %select_n.24), kind=kLoop, calls=%fused_computation.8 | loop fusion | bytes 1048580 | tf_op jit(solution)/shard_map/dynamic_slice | solution.py:450
  20.7 0.5 collective-permute-start.6
  21.3 0.8 fusion.2
  22.1 1.6 %collective-permute-start.2 = (f32[64,128]{1,0:T(8,128)S(1)}, f32[64,128]{1,0:T(8,128)S(1)}, u32[]{:S(2)}, u32[]{:S(2)}) collective-permute-start(f32[64,128]{1,0:T(8,128)S(1)} %fusion.2), channel_id=1, source_target_pairs={{0,2},{1,3},{2,0},{3,1},{4,6},{5,7},{6,4},{7,5},{8,10},{9,11},{10,... | collective-permute-start | bytes 98312 | tf_op jit(solution)/shard_map/ppermute | solution.py:433
  23.7 1.9 %constant_dynamic-slice_fusion.3 = f32[64,2048]{1,0:T(8,128)} fusion(f32[64,16384]{1,0:T(8,128)} %bitcast.9, s32[]{:T(128)S(6)} %select_n.25), kind=kLoop, calls=%fused_computation.7 | loop fusion | bytes 1048580 | tf_op jit(solution)/shard_map/dynamic_slice | solution.py:450
  25.6 1.5 %collective-permute-start.5 = (f32[64,2048]{1,0:T(8,128)}, f32[64,2048]{1,0:T(8,128)S(1)}, u32[]{:S(2)}, u32[]{:S(2)}) collective-permute-start(f32[64,2048]{1,0:T(8,128)} %constant_dynamic-slice_fusion.3), channel_id=1, source_target_pairs={{0,16},{8,24},{16,0},{24,8},{1,17},{9,25},{17,1},{25,9},{2,18},{10... | collective-permute-start | bytes 1572872 | tf_op jit(solution)/shard_map/ppermute | solution.py:425
  27.1 2.3 %constant_dynamic-slice_fusion.2 = f32[64,4096]{1,0:T(8,128)} fusion(f32[64,16384]{1,0:T(8,128)} %bitcast.10, s32[]{:T(128)S(6)} %select_n.26), kind=kLoop, calls=%fused_computation.6 | loop fusion | bytes 2097156 | tf_op jit(solution)/shard_map/dynamic_slice | solution.py:450
  29.3 0.5 collective-permute-start.16
  29.9 2.6 %collective-permute-start.3 = (f32[64,128]{1,0:T(8,128)S(1)}, f32[64,128]{1,0:T(8,128)S(1)}, u32[]{:S(2)}, u32[]{:S(2)}) collective-permute-start(f32[64,128]{1,0:T(8,128)S(1)} %add.62), channel_id=1, source_target_pairs={{0,4},{1,5},{2,6},{3,7},{4,0},{5,1},{6,2},{7,3},{8,12},{9,13},{10,... | collective-permute-start | bytes 98312 | tf_op jit(solution)/shard_map/ppermute | solution.py:433
  32.4 2.2 %collective-permute-done.3 = f32[64,128]{1,0:T(8,128)S(1)} collective-permute-done((f32[64,128]{1,0:T(8,128)S(1)}, f32[64,128]{1,0:T(8,128)S(1)}, u32[]{:S(2)}, u32[]{:S(2)}) %collective-permute-start.3) | collective-permute-done | bytes 32800 | tf_op jit(solution)/shard_map/ppermute | solution.py:433
  34.7 0.6 add.64.ref
  35.3 1.0 copy-done
  36.3 4.2 %shard_map.38.refs_3_ = f32[64,128]{1,0:T(8,128)} custom-call(s32[1]{0:T(128)} %bitcast.where.me_ref, f32[64,16384]{1,0:T(8,128)} %bitcast.11, f32[64,16384]{1,0:T(8,128)} %collective-permute-done.refs_1_, f32[64,4096]{1,0:T(8,128)} %copy-done), custom_call_target="tpu_custom_call" | custom-call | flops 603979776 | bytes 3145728 | tf_op jit(solution)/shard_map/pallas_call | solution.py:124
  40.5 6.8 %invert.1 = f32[64,128]{1,0:T(8,128)} custom-call(f32[64,128]{1,0:T(8,128)} %add.64.ref), custom_call_target="tpu_custom_call" | custom-call | flops 16384000 | bytes 65536 | tf_op jit(solution)/shard_map/invert/pallas_call | solution.py:156
  47.4 0.8 copy-done.2
  48.2 3.5 %shard_map.39.refs_3_ = f32[64,128]{1,0:T(8,128)} custom-call(s32[1]{0:T(128)} %bitcast.where.me_ref, f32[64,16384]{1,0:T(8,128)} %bitcast.12, f32[64,16384]{1,0:T(8,128)} %collective-permute-done.refs_1_, f32[64,2048]{1,0:T(8,128)} %copy-done.2, f32[64,128]{1,0:T(8,128)} %shard_map.38.refs_3_), custom_call_target="tpu_custom_call" | custom-call | flops 301989888 | bytes 1572864 | tf_op jit(solution)/shard_map/pallas_call | solution.py:124
  51.9 0.8 copy-done.4
  52.7 3.5 %shard_map.40 = f32[64,128]{1,0:T(8,128)} custom-call(s32[1]{0:T(128)} %bitcast.where.me_ref, f32[64,16384]{1,0:T(8,128)} %bitcast.13, f32[64,16384]{1,0:T(8,128)} %collective-permute-done.refs_1_, f32[64,2048]{1,0:T(8,128)} %copy-done.4, f32[64,128]{1,0:T(8,128)} %shard_map.39.refs_3_), custom_call_target="tpu_custom_call" | custom-call | flops 301989888 | bytes 1572864 | tf_op jit(solution)/shard_map/pallas_call | solution.py:124
  56.3 2.1 %collective-permute-start.7 = (f32[64,128]{1,0:T(8,128)}, f32[64,128]{1,0:T(8,128)S(1)}, u32[]{:S(2)}, u32[]{:S(2)}) collective-permute-start(f32[64,128]{1,0:T(8,128)} %shard_map.40), channel_id=1, source_target_pairs={{0,1},{1,0},{2,3},{3,2},{4,5},{5,4},{6,7},{7,6},{8,9},{9,8},{10,11... | collective-permute-start | bytes 98312 | tf_op jit(solution)/shard_map/ppermute | solution.py:433
  58.4 1.1 constant_dynamic-slice_fusion.1
  59.5 1.0 collective-permute-done.7
  60.5 0.8 add.68
  61.2 2.1 %collective-permute-start.8 = (f32[64,128]{1,0:T(8,128)S(1)}, f32[64,128]{1,0:T(8,128)S(1)}, u32[]{:S(2)}, u32[]{:S(2)}) collective-permute-start(f32[64,128]{1,0:T(8,128)S(1)} %add.68), channel_id=1, source_target_pairs={{0,2},{1,3},{2,0},{3,1},{4,6},{5,7},{6,4},{7,5},{8,10},{9,11},{10,... | collective-permute-start | bytes 98312 | tf_op jit(solution)/shard_map/ppermute | solution.py:433
  63.3 1.9 %constant_dynamic-slice_fusion = f32[64,2048]{1,0:T(8,128)} fusion(f32[64,16384]{1,0:T(8,128)} %bitcast.15, s32[]{:T(128)S(6)} %select_n.29), kind=kLoop, calls=%fused_computation.4 | loop fusion | bytes 1048580 | tf_op jit(solution)/shard_map/dynamic_slice | solution.py:450
  65.3 3.0 %collective-permute-start.9 = (f32[64,128]{1,0:T(8,128)S(1)}, f32[64,128]{1,0:T(8,128)S(1)}, u32[]{:S(2)}, u32[]{:S(2)}) collective-permute-start(f32[64,128]{1,0:T(8,128)S(1)} %add.71), channel_id=1, source_target_pairs={{0,4},{1,5},{2,6},{3,7},{4,0},{5,1},{6,2},{7,3},{8,12},{9,13},{10,... | collective-permute-start | bytes 98312 | tf_op jit(solution)/shard_map/ppermute | solution.py:433
  68.3 1.9 %collective-permute-done.9 = f32[64,128]{1,0:T(8,128)S(1)} collective-permute-done((f32[64,128]{1,0:T(8,128)S(1)}, f32[64,128]{1,0:T(8,128)S(1)}, u32[]{:S(2)}, u32[]{:S(2)}) %collective-permute-start.9) | collective-permute-done | bytes 32800 | tf_op jit(solution)/shard_map/ppermute | solution.py:433
  70.3 3.9 %collective-permute-done.16.refs_8_ = f32[64,4096]{1,0:T(8,128)S(1)} collective-permute-done((f32[64,4096]{1,0:T(8,128)}, f32[64,4096]{1,0:T(8,128)S(1)}, u32[]{:S(2)}, u32[]{:S(2)}) %collective-permute-start.16) | collective-permute-done | bytes 1048608 | tf_op jit(solution)/shard_map/ppermute | solution.py:425
  74.2 1.7 %collective-permute-start.19 = (f32[64,2048]{1,0:T(8,128)S(1)}, f32[64,2048]{1,0:T(8,128)S(1)}, u32[]{:S(2)}, u32[]{:S(2)}) collective-permute-start(f32[64,2048]{1,0:T(8,128)S(1)} %constant_dynamic-slice_fusion.1), channel_id=1, source_target_pairs={{0,16},{8,24},{16,0},{24,8},{1,17},{9,25},{17,1},{25,9},{2,18},{10... | collective-permute-start | bytes 1572872 | tf_op jit(solution)/shard_map/ppermute | solution.py:425
  76.0 0.3 collective-permute-start.10
  76.3 1.0 collective-permute-done.10
  77.3 1.5 %collective-permute-start.11 = (f32[256,128]{1,0:T(8,128)S(1)}, f32[256,128]{1,0:T(8,128)S(1)}, u32[]{:S(2)}, u32[]{:S(2)}) collective-permute-start(f32[256,128]{1,0:T(8,128)S(1)} %pad_maximum_fusion.refs_0_), channel_id=1, source_target_pairs={{0,16},{8,24},{16,0},{24,8},{1,17},{9,25},{17,1},{25,9},{2,18},{10... | collective-permute-start | bytes 393224 | tf_op jit(solution)/shard_map/ppermute | solution.py:425
  78.9 12.5 %collective-permute-done.11.refs_1_ = f32[256,128]{1,0:T(8,128)S(1)} collective-permute-done((f32[256,128]{1,0:T(8,128)S(1)}, f32[256,128]{1,0:T(8,128)S(1)}, u32[]{:S(2)}, u32[]{:S(2)}) %collective-permute-start.11) | collective-permute-done | bytes 131104 | tf_op jit(solution)/shard_map/ppermute | solution.py:425
  92.1 0.8 copy-done.7
  92.8 1.7 %collective-permute-start.12 = (f32[64,2048]{1,0:T(8,128)}, f32[64,2048]{1,0:T(8,128)}, u32[]{:S(2)}, u32[]{:S(2)}) collective-permute-start(f32[64,2048]{1,0:T(8,128)} %constant_dynamic-slice_fusion), channel_id=1, source_target_pairs={{0,16},{8,24},{16,0},{24,8},{1,17},{9,25},{17,1},{25,9},{2,18},{10... | collective-permute-start | bytes 1572872 | tf_op jit(solution)/shard_map/ppermute | solution.py:425
  94.6 9.8 %small.1.coeffs = f32[64,256]{1,0:T(8,128)} custom-call(s32[1]{0:T(128)} %bitcast.where.me_ref, s32[1]{0:T(128)S(6)} %copy.8.root_ref, s32[4]{0:T(128)} %code_ref.1, f32[256,128]{1,0:T(8,128)} %copy-done.11, f32[256,128]{1,0:T(8,128)} %copy-done.12), custom_call_target="tpu_custom_call" | custom-call | flops 5242880000 | bytes 262144 | tf_op jit(solution)/shard_map/small/pallas_call | solution.py:298
  104.7 0.5 copy-done.6
  105.2 8.4 %mix.3.refs_4_ = f32[64,16384]{1,0:T(8,128)} custom-call(s32[1]{0:T(128)} %bitcast.where.me_ref, f32[64,256]{1,0:T(8,128)} %small.1.coeffs, f32[64,16384]{1,0:T(8,128)} %bitcast.16, f32[64,16384]{1,0:T(8,128)} %collective-permute-done.refs_1_, f32[64,4096]{1,0:T(8,128)} %copy-done, f32[64,4096]{1,0:T(8,128)} %collective-permute-done.13.refs_3_, ...), custom_call_target="tpu_custom_call" | custom-call | flops 2415919104 | bytes 15728640 | tf_op jit(solution)/shard_map/mix/pallas_call | solution.py:374
  113.9 0.8 copy-done.8
  114.8 3.7 %mix.4.refs_4_ = f32[64,16384]{1,0:T(8,128)} custom-call(s32[1]{0:T(128)} %bitcast.where.me_ref, f32[64,256]{1,0:T(8,128)} %small.1.coeffs, f32[64,16384]{1,0:T(8,128)} %bitcast.17, f32[64,16384]{1,0:T(8,128)} %collective-permute-done.refs_1_, f32[64,2048]{1,0:T(8,128)} %copy-done.7, f32[64,2048]{1,0:T(8,128)} %copy-done.8, ...), custom_call_target="tpu_custom_call", output_to_operand_aliasing={{}: (6, {})} | custom-call | flops 402653184 | bytes 2621440 | tf_op jit(solution)/shard_map/mix/pallas_call | solution.py:374
  118.5 0.8 copy-done.9
  119.3 3.7 %mix.5 = f32[64,16384]{1,0:T(8,128)} custom-call(s32[1]{0:T(128)} %bitcast.where.me_ref, f32[64,256]{1,0:T(8,128)} %small.1.coeffs, f32[64,16384]{1,0:T(8,128)} %bitcast.18, f32[64,16384]{1,0:T(8,128)} %collective-permute-done.refs_1_, f32[64,2048]{1,0:T(8,128)} %collective-permute-done.12.refs_2_, ...), custom_call_target="tpu_custom_call", output_to_operand_aliasing={{}: (6, {})} | custom-call | flops 402653184 | bytes 2621440 | tf_op jit(solution)/shard_map/mix/pallas_call | solution.py:374
  (45 shorter events, 1.0 us)
Async XLA Ops:
  0.0 12.2 %collective-permute-start = (f32[64,16384]{1,0:T(8,128)}, f32[64,16384]{1,0:T(8,128)}, u32[]{:S(2)}, u32[]{:S(2)}) collective-permute-start(f32[64,16384]{1,0:T(8,128)} %bitcast.6), channel_id=1, source_target_pairs={{0,8},{8,0},{16,24},{24,16},{1,9},{9,1},{17,25},{25,17},{2,10},{10... | collective-permute-start | bytes 12582920 | tf_op jit(solution)/shard_map/ppermute | solution.py:425
  2.8 32.5 %collective-permute-start.4 = (f32[64,4096]{1,0:T(8,128)}, f32[64,4096]{1,0:T(8,128)S(1)}, u32[]{:S(2)}, u32[]{:S(2)}) collective-permute-start(f32[64,4096]{1,0:T(8,128)} %dynamic-slice_bitcast_fusion), channel_id=1, source_target_pairs={{0,16},{8,24},{16,0},{24,8},{1,17},{9,25},{17,1},{25,9},{2,18},{10... | collective-permute-start | bytes 3145736 | tf_op jit(solution)/shard_map/ppermute | solution.py:425
  17.3 3.9 %collective-permute-start.1 = (f32[64,128]{1,0:T(8,128)S(1)}, f32[64,128]{1,0:T(8,128)S(1)}, u32[]{:S(2)}, u32[]{:S(2)}) collective-permute-start(f32[64,128]{1,0:T(8,128)S(1)} %pad_maximum_fusion.2), channel_id=1, source_target_pairs={{0,1},{1,0},{2,3},{3,2},{4,5},{5,4},{6,7},{7,6},{8,9},{9,8},{10,11... | collective-permute-start | bytes 98312 | tf_op jit(solution)/shard_map/ppermute | solution.py:433
  20.7 26.6 %collective-permute-start.6 = (f32[64,2048]{1,0:T(8,128)}, f32[64,2048]{1,0:T(8,128)S(1)}, u32[]{:S(2)}, u32[]{:S(2)}) collective-permute-start(f32[64,2048]{1,0:T(8,128)} %constant_dynamic-slice_fusion.4), channel_id=1, source_target_pairs={{0,16},{8,24},{16,0},{24,8},{1,17},{9,25},{17,1},{25,9},{2,18},{10... | collective-permute-start | bytes 1572872 | tf_op jit(solution)/shard_map/ppermute | solution.py:425
  22.1 5.0 %collective-permute-start.2 = (f32[64,128]{1,0:T(8,128)S(1)}, f32[64,128]{1,0:T(8,128)S(1)}, u32[]{:S(2)}, u32[]{:S(2)}) collective-permute-start(f32[64,128]{1,0:T(8,128)S(1)} %fusion.2), channel_id=1, source_target_pairs={{0,2},{1,3},{2,0},{3,1},{4,6},{5,7},{6,4},{7,5},{8,10},{9,11},{10,... | collective-permute-start | bytes 98312 | tf_op jit(solution)/shard_map/ppermute | solution.py:433
  25.6 26.4 %collective-permute-start.5 = (f32[64,2048]{1,0:T(8,128)}, f32[64,2048]{1,0:T(8,128)S(1)}, u32[]{:S(2)}, u32[]{:S(2)}) collective-permute-start(f32[64,2048]{1,0:T(8,128)} %constant_dynamic-slice_fusion.3), channel_id=1, source_target_pairs={{0,16},{8,24},{16,0},{24,8},{1,17},{9,25},{17,1},{25,9},{2,18},{10... | collective-permute-start | bytes 1572872 | tf_op jit(solution)/shard_map/ppermute | solution.py:425
  29.3 44.9 %collective-permute-start.16 = (f32[64,4096]{1,0:T(8,128)}, f32[64,4096]{1,0:T(8,128)S(1)}, u32[]{:S(2)}, u32[]{:S(2)}) collective-permute-start(f32[64,4096]{1,0:T(8,128)} %constant_dynamic-slice_fusion.2), channel_id=1, source_target_pairs={{0,16},{8,24},{16,0},{24,8},{1,17},{9,25},{17,1},{25,9},{2,18},{10... | collective-permute-start | bytes 3145736 | tf_op jit(solution)/shard_map/ppermute | solution.py:425
  29.9 4.8 %collective-permute-start.3 = (f32[64,128]{1,0:T(8,128)S(1)}, f32[64,128]{1,0:T(8,128)S(1)}, u32[]{:S(2)}, u32[]{:S(2)}) collective-permute-start(f32[64,128]{1,0:T(8,128)S(1)} %add.62), channel_id=1, source_target_pairs={{0,4},{1,5},{2,6},{3,7},{4,0},{5,1},{6,2},{7,3},{8,12},{9,13},{10,... | collective-permute-start | bytes 98312 | tf_op jit(solution)/shard_map/ppermute | solution.py:433
  35.3 1.0 copy-start
  47.4 0.8 copy-start.2
  51.7 18.5 %copy-start.1 = (f32[64,4096]{1,0:T(8,128)S(1)}, f32[64,4096]{1,0:T(8,128)}, u32[]{:S(2)}) copy-start(f32[64,4096]{1,0:T(8,128)} %copy-done) | copy-start | bytes 3145732
  51.7 24.3 %copy-start.10 = (f32[64,128]{1,0:T(8,128)S(1)}, f32[64,128]{1,0:T(8,128)}, u32[]{:S(2)}) copy-start(f32[64,128]{1,0:T(8,128)} %invert.1) | copy-start | bytes 98308
  51.7 27.2 %copy-start.3 = (f32[64,2048]{1,0:T(8,128)S(1)}, f32[64,2048]{1,0:T(8,128)}, u32[]{:S(2)}) copy-start(f32[64,2048]{1,0:T(8,128)} %copy-done.2) | copy-start | bytes 1572868
  51.9 0.8 copy-start.4
  56.3 4.2 %collective-permute-start.7 = (f32[64,128]{1,0:T(8,128)}, f32[64,128]{1,0:T(8,128)S(1)}, u32[]{:S(2)}, u32[]{:S(2)}) collective-permute-start(f32[64,128]{1,0:T(8,128)} %shard_map.40), channel_id=1, source_target_pairs={{0,1},{1,0},{2,3},{3,2},{4,5},{5,4},{6,7},{7,6},{8,9},{9,8},{10,11... | collective-permute-start | bytes 98312 | tf_op jit(solution)/shard_map/ppermute | solution.py:433
  61.2 4.0 %collective-permute-start.8 = (f32[64,128]{1,0:T(8,128)S(1)}, f32[64,128]{1,0:T(8,128)S(1)}, u32[]{:S(2)}, u32[]{:S(2)}) collective-permute-start(f32[64,128]{1,0:T(8,128)S(1)} %add.68), channel_id=1, source_target_pairs={{0,2},{1,3},{2,0},{3,1},{4,6},{5,7},{6,4},{7,5},{8,10},{9,11},{10,... | collective-permute-start | bytes 98312 | tf_op jit(solution)/shard_map/ppermute | solution.py:433
  65.3 4.9 %collective-permute-start.9 = (f32[64,128]{1,0:T(8,128)S(1)}, f32[64,128]{1,0:T(8,128)S(1)}, u32[]{:S(2)}, u32[]{:S(2)}) collective-permute-start(f32[64,128]{1,0:T(8,128)S(1)} %add.71), channel_id=1, source_target_pairs={{0,4},{1,5},{2,6},{3,7},{4,0},{5,1},{6,2},{7,3},{8,12},{9,13},{10,... | collective-permute-start | bytes 98312 | tf_op jit(solution)/shard_map/ppermute | solution.py:433
  70.2 34.5 %collective-permute-start.13 = (f32[64,4096]{1,0:T(8,128)S(1)}, f32[64,4096]{1,0:T(8,128)}, u32[]{:S(2)}, u32[]{:S(2)}) collective-permute-start(f32[64,4096]{1,0:T(8,128)S(1)} %copy-done.1), channel_id=1, source_target_pairs={{0,8},{8,0},{16,24},{24,16},{1,9},{9,1},{17,25},{25,17},{2,10},{10... | collective-permute-start | bytes 3145736 | tf_op jit(solution)/shard_map/ppermute | solution.py:425
  74.2 30.2 %copy-start.5 = (f32[64,4096]{1,0:T(8,128)}, f32[64,4096]{1,0:T(8,128)S(1)}, u32[]{:S(2)}) copy-start(f32[64,4096]{1,0:T(8,128)S(1)} %collective-permute-done.16.refs_8_) | copy-start | bytes 3145732
  74.2 30.5 %collective-permute-start.17 = (f32[64,4096]{1,0:T(8,128)S(1)}, f32[64,4096]{1,0:T(8,128)}, u32[]{:S(2)}, u32[]{:S(2)}) collective-permute-start(f32[64,4096]{1,0:T(8,128)S(1)} %collective-permute-done.16.refs_8_), channel_id=1, source_target_pairs={{0,8},{8,0},{16,24},{24,16},{1,9},{9,1},{17,25},{25,17},{2,10},{10... | collective-permute-start | bytes 3145736 | tf_op jit(solution)/shard_map/ppermute | solution.py:425
  74.2 17.8 %collective-permute-start.19 = (f32[64,2048]{1,0:T(8,128)S(1)}, f32[64,2048]{1,0:T(8,128)S(1)}, u32[]{:S(2)}, u32[]{:S(2)}) collective-permute-start(f32[64,2048]{1,0:T(8,128)S(1)} %constant_dynamic-slice_fusion.1), channel_id=1, source_target_pairs={{0,16},{8,24},{16,0},{24,8},{1,17},{9,25},{17,1},{25,9},{2,18},{10... | collective-permute-start | bytes 1572872 | tf_op jit(solution)/shard_map/ppermute | solution.py:425
  76.0 1.3 %collective-permute-start.10 = (f32[128,128]{1,0:T(8,128)S(1)}, f32[128,128]{1,0:T(8,128)S(1)}, u32[]{:S(2)}, u32[]{:S(2)}) collective-permute-start(f32[128,128]{1,0:T(8,128)S(1)} %pad_maximum_fusion.1), channel_id=1, source_target_pairs={{0,8},{8,0},{16,24},{24,16},{1,9},{9,1},{17,25},{25,17},{2,10},{10... | collective-permute-start | bytes 196616 | tf_op jit(solution)/shard_map/ppermute | solution.py:425
  77.3 17.3 %copy-start.11 = (f32[256,128]{1,0:T(8,128)}, f32[256,128]{1,0:T(8,128)S(1)}, u32[]{:S(2)}) copy-start(f32[256,128]{1,0:T(8,128)S(1)} %pad_maximum_fusion.refs_0_) | copy-start | bytes 393220
  77.3 14.0 %collective-permute-start.11 = (f32[256,128]{1,0:T(8,128)S(1)}, f32[256,128]{1,0:T(8,128)S(1)}, u32[]{:S(2)}, u32[]{:S(2)}) collective-permute-start(f32[256,128]{1,0:T(8,128)S(1)} %pad_maximum_fusion.refs_0_), channel_id=1, source_target_pairs={{0,16},{8,24},{16,0},{24,8},{1,17},{9,25},{17,1},{25,9},{2,18},{10... | collective-permute-start | bytes 393224 | tf_op jit(solution)/shard_map/ppermute | solution.py:425
  78.9 25.5 %collective-permute-start.14 = (f32[64,2048]{1,0:T(8,128)S(1)}, f32[64,2048]{1,0:T(8,128)S(1)}, u32[]{:S(2)}, u32[]{:S(2)}) collective-permute-start(f32[64,2048]{1,0:T(8,128)S(1)} %copy-done.3), channel_id=1, source_target_pairs={{0,8},{8,0},{16,24},{24,16},{1,9},{9,1},{17,25},{25,17},{2,10},{10... | collective-permute-start | bytes 1572872 | tf_op jit(solution)/shard_map/ppermute | solution.py:425
  91.4 3.2 %copy-start.12 = (f32[256,128]{1,0:T(8,128)}, f32[256,128]{1,0:T(8,128)S(1)}, u32[]{:S(2)}) copy-start(f32[256,128]{1,0:T(8,128)S(1)} %collective-permute-done.11.refs_1_) | copy-start | bytes 393220
  91.4 13.3 %collective-permute-start.15 = (f32[64,2048]{1,0:T(8,128)}, f32[64,2048]{1,0:T(8,128)}, u32[]{:S(2)}, u32[]{:S(2)}) collective-permute-start(f32[64,2048]{1,0:T(8,128)} %copy-done.4), channel_id=1, source_target_pairs={{0,8},{8,0},{16,24},{24,16},{1,9},{9,1},{17,25},{25,17},{2,10},{10... | collective-permute-start | bytes 1572872 | tf_op jit(solution)/shard_map/ppermute | solution.py:425
  92.0 0.8 copy-start.7
  92.8 20.8 %collective-permute-start.12 = (f32[64,2048]{1,0:T(8,128)}, f32[64,2048]{1,0:T(8,128)}, u32[]{:S(2)}, u32[]{:S(2)}) collective-permute-start(f32[64,2048]{1,0:T(8,128)} %constant_dynamic-slice_fusion), channel_id=1, source_target_pairs={{0,16},{8,24},{16,0},{24,8},{1,17},{9,25},{17,1},{25,9},{2,18},{10... | collective-permute-start | bytes 1572872 | tf_op jit(solution)/shard_map/ppermute | solution.py:425
  104.4 0.8 copy-start.6
  104.4 9.5 %collective-permute-start.20 = (f32[64,2048]{1,0:T(8,128)}, f32[64,2048]{1,0:T(8,128)S(1)}, u32[]{:S(2)}, u32[]{:S(2)}) collective-permute-start(f32[64,2048]{1,0:T(8,128)} %copy-done.7), channel_id=1, source_target_pairs={{0,8},{8,0},{16,24},{24,16},{1,9},{9,1},{17,25},{25,17},{2,10},{10... | collective-permute-start | bytes 1572872 | tf_op jit(solution)/shard_map/ppermute | solution.py:425
  113.6 4.8 %collective-permute-start.18 = (f32[64,2048]{1,0:T(8,128)}, f32[64,2048]{1,0:T(8,128)S(1)}, u32[]{:S(2)}, u32[]{:S(2)}) collective-permute-start(f32[64,2048]{1,0:T(8,128)} %collective-permute-done.12.refs_2_), channel_id=1, source_target_pairs={{0,8},{8,0},{16,24},{24,16},{1,9},{9,1},{17,25},{25,17},{2,10},{10... | collective-permute-start | bytes 1572872 | tf_op jit(solution)/shard_map/ppermute | solution.py:425
  113.9 0.8 copy-start.8
  118.4 0.8 copy-start.9

commit v3 on v2

--- a/solution.py
+++ b/solution.py
@@ -16,7 +16,8 @@
 
 CORES = 2
 LOWEST = 1.0 / 1.64
-STEP = 6
+STEP = 8
+GRANT = 67043328
 
 
 def xor_pairs(size, offset):
@@ -89,8 +90,8 @@
     count = (len(refs) - 2 - (1 if prior else 0)) // 2
     loaded, out = refs[:count], refs[count + (1 if prior else 0)]
     slots, sems = refs[-1 - count:-1], refs[-1]
-    size, extent = slots[0].shape
-    start = at(where) * extent
+    size, _ = slots[0].shape
+    start = at(where)
     waits = load(loaded, [start] * whole + [0] * (count - whole), slots, sems, tile)
     totals = [None] * len(heads)
     for t, copies in enumerate(waits):
@@ -110,7 +111,7 @@
     out[...] = result + refs[count][...] if prior else result
 
 
-def gram(where, at, whole, parts, heads, groups, before, extent, tile):
+def gram(where, at, whole, parts, heads, groups, before, extent, tile, grant):
     size = (whole + parts)[0].shape[0]
     tile = min(tile, extent)
     width = sum(len(columns) for columns in groups) * size
@@ -132,6 +133,7 @@
             flops=9 * 2 * size * width * extent, transcendentals=0,
             bytes_accessed=4 * count * size * extent,
         ),
+        compiler_params=pltpu.CompilerParams(vmem_limit_bytes=grant),
     )(where, *operands)
 
 
@@ -383,6 +385,7 @@
             flops=6 * 2 * n * size * size * extent, transcendentals=0,
             bytes_accessed=4 * (n + 1) * size * extent,
         ),
+        compiler_params=pltpu.CompilerParams(vmem_limit_bytes=GRANT),
         name="mix",
     )(*operands)
 
@@ -392,7 +395,7 @@
 
 
 def widths(chips):
-    return ((8, 4, 4), (8, 4, 4)) if chips == 2 else ((16,), (8, 8))
+    return ((8, 6, 2), (8, 6, 2)) if chips == 2 else ((16,), (8, 8))
 
 
 def early_of(chips):
@@ -471,13 +474,13 @@
         return piece
 
     pair_gram = gram(
-        where, lambda w: w[0] % CORES, [own, partner], [], [0], [(1,)], None, cols // CORES, 2048
+        where, lambda w: w[0] % CORES * (cols // CORES), [own, partner], [], [0], [(1,)], None, cols // CORES, 2048, GRANT
     )
     calls = [lambda x, c=c: send_near(c, after(own, x)) for c in range(1, len(near_widths))]
     calls += [lambda x, key=key: send_far(*key, after(own, x)) for key in early]
     own_gram = mesh_sum(jnp.concatenate([own_gram, pair_gram], axis=1), calls)
 
-    cross, others = None, {}
+    cross, others, crosses = None, {}, []
     ready = invert(own_gram) if len(near_widths) == 1 else own_gram
     for c, (start, width) in enumerate(zip(near_starts, near_widths)):
         dep = ready if cross is None else cross
@@ -495,9 +498,11 @@
         for o in range(1, chips - 1):
             groups.append(groups[-1] + (heads_at[o - 1], CORES + chips - 1 + o - 1))
         cross = gram(
-            where, lambda w, start=start, width=width: (w[0] // CORES * 16 + start) // width,
+            where, lambda w, start=start: w[0] // CORES * part + start * unit,
             [own, partner], heads + columns, heads_at, groups, cross, width * unit, 1024,
+            GRANT if c < len(near_widths) - 1 else None,
         )
+        crosses.append(cross)
     late = [key for key in far_names(chips) if key not in early]
     cross = mesh_sum(cross, [lambda x, key=key: send_far(*key, after(own, x)) for key in late])
     width = max(cross.shape[1], ready.shape[1])
@@ -521,19 +526,17 @@
     for c in range(len(near_widths)):
         parts = []
         for o in range(1, chips):
-            other = others[o, c] if (o, c) in others else forward(near[o, c], cross)
+            other = others[o, c] if (o, c) in others else forward(near[o, c], crosses[c])
             parts += [near[o, c], other]
         chunks.append((at_near(near_starts[c]), parts))
     places = [(p, c) for p in range(1, chips) for c in range(len(far_widths))]
     first = [(p, c) for p, c in places if all((o, p, c) in early for o in range(1, chips))]
-    chunks += [far_parts(p, c, cross) for p, c in first]
     result = mix(where, coeffs, [own, partner], chunks, None, 2 * unit)
     results = [coeffs, result]
     for p, c in places:
-        if (p, c) not in first:
-            chunk = far_parts(p, c, results[-2])
-            result = mix(where, coeffs, [own, partner], [chunk], result, 2 * unit)
-            results.append(result)
+        chunk = far_parts(p, c, cross if (p, c) in first else results[-2])
+        result = mix(where, coeffs, [own, partner], [chunk], result, 2 * unit)
+        results.append(result)
     return result
 
 

time: 124 us -> 128 us (1.032)
  waiting for transfers between devices: 22.9 us -> 28.5 us
  local copies, waits for them, and re-layouts: 16.9 us -> 12.8 us
  Pallas kernels: 47.9 us -> 50.7 us
    ppermute x15, waiting for transfers between devices: 17.8 us -> 26.3 us  [move(): return lax.ppermute(x, 'variant', xor_pairs(n, offset))]
    unnamed x26 -> x6, local copies, waits for them, and re-layouts: 5.58 us -> 0.64 us
    ppermute x6, waiting for transfers between devices: 5.15 us -> 2.14 us  [mesh_sum(): arrived = lax.ppermute(x, 'mesh', xor_pairs(mesh_size, step))]
    pallas_call x3 -> x4, Pallas kernels: 15.8 us -> 18.5 us  [mix(): pl.pallas_call(functools.partial(mix_kernel, len(whole), layout, tile, le...]
  transfers between devices with their start and end apart: 21 -> 21, of which waited for: 7 -> 7; matrix products, arithmetic and copies ran while one was open for 17% -> 18% of each run, Pallas kernels for 36% -> 37%
where the time goes in v3:
time: 128 us; the launch traced here: 127 us
  Pallas kernels  50.7 us (40%)
  waiting for transfers between devices  28.5 us (22%)
  starting transfers between devices  23.7 us (19%)
  local copies, waits for them, and re-layouts  12.8 us (10%)
  matrix products  7.55 us (6%)
  other arithmetic  3.11 us (2%)
    ppermute x15, waiting for transfers between devices, move(): return lax.ppermute(x, 'variant', xor_pairs(n, offset))  26.3 us
    pallas_call x4, Pallas kernels, mix(): pl.pallas_call(functools.partial(mix_kernel, len(whole), layout, tile, le...  18.5 us
    pallas_call x4, Pallas kernels, gram(): pl.pallas_call(functools.partial(gram_kernel, heads, groups, before is no...  15.8 us
    ppermute x6, starting transfers between devices, mesh_sum(): arrived = lax.ppermute(x, 'mesh', xor_pairs(mesh_size, step))  13 us
    dynamic_slice x6, local copies, waits for them, and re-layouts, piece_of(): lax.dynamic_slice(x, (0, (chip ^ offset) * part + start * unit), (size, w...  12.1 us
    ppermute x15, starting transfers between devices, move(): return lax.ppermute(x, 'variant', xor_pairs(n, offset))  10.7 us
    pallas_call x1, Pallas kernels, small(): pl.pallas_call(functools.partial(small_kernel, n, scale), out_shape=jax.S...  9.52 us
    dot_general x1, matrix products, mmt(): lax.dot_general(a, b, (((1,), (1,)), ((), ())), precision=highest, prefer...  7.55 us
  transfers between devices with their start and end apart: 21, of which 7 were waited for; matrix products, arithmetic and copies ran while one was open for 18% of the time, Pallas kernels for 37%

profile of v3, /device:TPU:0, one launch (start us, length us, event | category | flops | bytes accessed | tf_op | source)
XLA Modules:
  0.0 127.3 jit_solution(8689945369378907225)
XLA Ops:
  0.0 0.5 collective-permute-start
  0.5 2.3 %dynamic-slice_bitcast_fusion = f32[64,4096]{1,0:T(8,128)} fusion(f32[1,64,16384]{2,1,0:T(8,128)} %param.3, s32[]{:T(128)S(6)} %select_n.27), kind=kLoop, calls=%fused_computation | loop fusion | bytes 2097156 | tf_op jit(solution)/shard_map/dynamic_slice | solution.py:453
  2.8 2.5 %collective-permute-start.4 = (f32[64,4096]{1,0:T(8,128)}, f32[64,4096]{1,0:T(8,128)}, u32[]{:S(2)}, u32[]{:S(2)}) collective-permute-start(f32[64,4096]{1,0:T(8,128)} %dynamic-slice_bitcast_fusion), channel_id=1, source_target_pairs={{0,16},{8,24},{16,0},{24,8},{1,17},{9,25},{17,1},{25,9},{2,18},{10... | collective-permute-start | bytes 3145736 | tf_op jit(solution)/shard_map/ppermute | solution.py:428
  5.2 7.5 %fusion = f32[64,64]{1,0:T(8,128)} fusion(f32[1,64,16384]{2,1,0:T(8,128)} %param.3), kind=kOutput, calls=%fused_computation.9 | convolution fusion | flops 805306368 | bytes 4210688 | tf_op jit(solution)/shard_map/dot_general | solution.py:32
  12.8 4.3 %shard_map.37 = f32[64,64]{1,0:T(8,128)} custom-call(s32[1]{0:T(128)} %bitcast.where.me_ref, f32[64,16384]{1,0:T(8,128)} %bitcast.7, f32[64,16384]{1,0:T(8,128)} %collective-permute-done.refs_1_), custom_call_target="tpu_custom_call" | custom-call | flops 603979776 | bytes 4194304 | tf_op jit(solution)/shard_map/pallas_call | solution.py:125
  17.1 0.9 pad_maximum_fusion.2
  17.9 1.5 %collective-permute-start.1 = (f32[64,128]{1,0:T(8,128)S(1)}, f32[64,128]{1,0:T(8,128)S(1)}, u32[]{:S(2)}, u32[]{:S(2)}) collective-permute-start(f32[64,128]{1,0:T(8,128)S(1)} %pad_maximum_fusion.2), channel_id=1, source_target_pairs={{0,1},{1,0},{2,3},{3,2},{4,5},{5,4},{6,7},{7,6},{8,9},{9,8},{10,11... | collective-permute-start | bytes 98312 | tf_op jit(solution)/shard_map/ppermute | solution.py:436
  19.5 2.1 %constant_dynamic-slice_fusion.4 = f32[64,3072]{1,0:T(8,128)} fusion(f32[64,16384]{1,0:T(8,128)} %bitcast.8, s32[]{:T(128)S(6)} %select_n.24), kind=kLoop, calls=%fused_computation.8 | loop fusion | bytes 1572868 | tf_op jit(solution)/shard_map/dynamic_slice | solution.py:453
  21.5 0.5 collective-permute-start.6
  22.1 0.0 collective-permute-done.1
  22.1 0.9 fusion.2
  22.9 1.6 %collective-permute-start.2 = (f32[64,128]{1,0:T(8,128)S(1)}, f32[64,128]{1,0:T(8,128)S(1)}, u32[]{:S(2)}, u32[]{:S(2)}) collective-permute-start(f32[64,128]{1,0:T(8,128)S(1)} %fusion.2), channel_id=1, source_target_pairs={{0,2},{1,3},{2,0},{3,1},{4,6},{5,7},{6,4},{7,5},{8,10},{9,11},{10,... | collective-permute-start | bytes 98312 | tf_op jit(solution)/shard_map/ppermute | solution.py:436
  24.5 1.7 %constant_dynamic-slice_fusion.3 = f32[64,1024]{1,0:T(8,128)} fusion(f32[64,16384]{1,0:T(8,128)} %bitcast.9, s32[]{:T(128)S(6)} %select_n.25), kind=kLoop, calls=%fused_computation.7 | loop fusion | bytes 524292 | tf_op jit(solution)/shard_map/dynamic_slice | solution.py:453
  26.2 1.5 %collective-permute-start.5 = (f32[64,1024]{1,0:T(8,128)}, f32[64,1024]{1,0:T(8,128)}, u32[]{:S(2)}, u32[]{:S(2)}) collective-permute-start(f32[64,1024]{1,0:T(8,128)} %constant_dynamic-slice_fusion.3), channel_id=1, source_target_pairs={{0,16},{8,24},{16,0},{24,8},{1,17},{9,25},{17,1},{25,9},{2,18},{10... | collective-permute-start | bytes 786440 | tf_op jit(solution)/shard_map/ppermute | solution.py:428
  27.7 2.7 %collective-permute-start.3 = (f32[64,128]{1,0:T(8,128)S(1)}, f32[64,128]{1,0:T(8,128)S(1)}, u32[]{:S(2)}, u32[]{:S(2)}) collective-permute-start(f32[64,128]{1,0:T(8,128)S(1)} %add.62), channel_id=1, source_target_pairs={{0,4},{1,5},{2,6},{3,7},{4,0},{5,1},{6,2},{7,3},{8,12},{9,13},{10,... | collective-permute-start | bytes 98312 | tf_op jit(solution)/shard_map/ppermute | solution.py:436
  30.3 2.4 %constant_dynamic-slice_fusion.2 = f32[64,4096]{1,0:T(8,128)} fusion(f32[64,16384]{1,0:T(8,128)} %bitcast.10, s32[]{:T(128)S(6)} %select_n.26), kind=kLoop, calls=%fused_computation.6 | loop fusion | bytes 2097156 | tf_op jit(solution)/shard_map/dynamic_slice | solution.py:453
  32.7 0.6 collective-permute-start.13
  33.3 0.6 add.64.ref
  33.9 4.2 %shard_map.38.refs_3_ = f32[64,128]{1,0:T(8,128)} custom-call(s32[1]{0:T(128)} %bitcast.where.me_ref, f32[64,16384]{1,0:T(8,128)} %bitcast.11, f32[64,16384]{1,0:T(8,128)} %collective-permute-done.refs_1_, f32[64,4096]{1,0:T(8,128)} %collective-permute-done.4.refs_2_), custom_call_target="tpu_custom_call" | custom-call | flops 603979776 | bytes 3145728 | tf_op jit(solution)/shard_map/pallas_call | solution.py:125
  38.1 6.8 %invert.1 = f32[64,128]{1,0:T(8,128)} custom-call(f32[64,128]{1,0:T(8,128)} %add.64.ref), custom_call_target="tpu_custom_call" | custom-call | flops 16384000 | bytes 65536 | tf_op jit(solution)/shard_map/invert/pallas_call | solution.py:158
  45.0 1.5 %collective-permute-done.6.refs_2_.refs_4_ = f32[64,3072]{1,0:T(8,128)} collective-permute-done((f32[64,3072]{1,0:T(8,128)}, f32[64,3072]{1,0:T(8,128)}, u32[]{:S(2)}, u32[]{:S(2)}) %collective-permute-start.6) | collective-permute-done | bytes 786464 | tf_op jit(solution)/shard_map/ppermute | solution.py:428
  46.4 4.3 %shard_map.39.refs_3_ = f32[64,128]{1,0:T(8,128)} custom-call(s32[1]{0:T(128)} %bitcast.where.me_ref, f32[64,16384]{1,0:T(8,128)} %bitcast.12, f32[64,16384]{1,0:T(8,128)} %collective-permute-done.refs_1_, f32[64,3072]{1,0:T(8,128)} %collective-permute-done.6.refs_2_.refs_4_, f32[64,128]{1,0:T(8,128)} %shard_map.38.refs_3_), custom_call_target="tpu_custom_call" | custom-call | flops 452984832 | bytes 2359296 | tf_op jit(solution)/shard_map/pallas_call | solution.py:125
  50.7 1.3 %collective-permute-done.5.refs_2_.refs_6_ = f32[64,1024]{1,0:T(8,128)} collective-permute-done((f32[64,1024]{1,0:T(8,128)}, f32[64,1024]{1,0:T(8,128)}, u32[]{:S(2)}, u32[]{:S(2)}) %collective-permute-start.5) | collective-permute-done | bytes 262176 | tf_op jit(solution)/shard_map/ppermute | solution.py:428
  52.0 3.0 %shard_map.40 = f32[64,128]{1,0:T(8,128)} custom-call(s32[1]{0:T(128)} %bitcast.where.me_ref, f32[64,16384]{1,0:T(8,128)} %bitcast.13, f32[64,16384]{1,0:T(8,128)} %collective-permute-done.refs_1_, f32[64,1024]{1,0:T(8,128)} %collective-permute-done.5.refs_2_.refs_6_, f32[64,128]{1,0:T(8,128)} %shard_map.39.refs_3_), custom_call_target="tpu_custom_call" | custom-call | flops 150994944 | bytes 786432 | tf_op jit(solution)/shard_map/pallas_call | solution.py:125
  55.1 2.1 %collective-permute-start.7 = (f32[64,128]{1,0:T(8,128)}, f32[64,128]{1,0:T(8,128)S(1)}, u32[]{:S(2)}, u32[]{:S(2)}) collective-permute-start(f32[64,128]{1,0:T(8,128)} %shard_map.40), channel_id=1, source_target_pairs={{0,1},{1,0},{2,3},{3,2},{4,5},{5,4},{6,7},{7,6},{8,9},{9,8},{10,11... | collective-permute-start | bytes 98312 | tf_op jit(solution)/shard_map/ppermute | solution.py:436
  57.2 2.1 %constant_dynamic-slice_fusion.1 = f32[64,3072]{1,0:T(8,128)} fusion(f32[64,16384]{1,0:T(8,128)} %bitcast.14, s32[]{:T(128)S(6)} %select_n.28), kind=kLoop, calls=%fused_computation.5 | loop fusion | bytes 1572868 | tf_op jit(solution)/shard_map/dynamic_slice | solution.py:453
  59.3 0.8 add.68
  60.1 2.1 %collective-permute-start.8 = (f32[64,128]{1,0:T(8,128)S(1)}, f32[64,128]{1,0:T(8,128)S(1)}, u32[]{:S(2)}, u32[]{:S(2)}) collective-permute-start(f32[64,128]{1,0:T(8,128)S(1)} %add.68), channel_id=1, source_target_pairs={{0,2},{1,3},{2,0},{3,1},{4,6},{5,7},{6,4},{7,5},{8,10},{9,11},{10,... | collective-permute-start | bytes 98312 | tf_op jit(solution)/shard_map/ppermute | solution.py:436
  62.2 1.7 %constant_dynamic-slice_fusion = f32[64,1024]{1,0:T(8,128)} fusion(f32[64,16384]{1,0:T(8,128)} %bitcast.15, s32[]{:T(128)S(6)} %select_n.29), kind=kLoop, calls=%fused_computation.4 | loop fusion | bytes 524292 | tf_op jit(solution)/shard_map/dynamic_slice | solution.py:453
  63.8 0.2 collective-permute-done.8
  64.0 3.0 %collective-permute-start.9 = (f32[64,128]{1,0:T(8,128)S(1)}, f32[64,128]{1,0:T(8,128)S(1)}, u32[]{:S(2)}, u32[]{:S(2)}) collective-permute-start(f32[64,128]{1,0:T(8,128)S(1)} %add.71), channel_id=1, source_target_pairs={{0,4},{1,5},{2,6},{3,7},{4,0},{5,1},{6,2},{7,3},{8,12},{9,13},{10,... | collective-permute-start | bytes 98312 | tf_op jit(solution)/shard_map/ppermute | solution.py:436
  67.1 1.9 %collective-permute-done.9 = f32[64,128]{1,0:T(8,128)S(1)} collective-permute-done((f32[64,128]{1,0:T(8,128)S(1)}, f32[64,128]{1,0:T(8,128)S(1)}, u32[]{:S(2)}, u32[]{:S(2)}) %collective-permute-start.9) | collective-permute-done | bytes 32800 | tf_op jit(solution)/shard_map/ppermute | solution.py:436
  69.0 0.1 collective-permute-start.10
  69.1 0.5 collective-permute-start.16
  69.6 1.8 %collective-permute-start.19 = (f32[64,3072]{1,0:T(8,128)}, f32[64,3072]{1,0:T(8,128)}, u32[]{:S(2)}, u32[]{:S(2)}) collective-permute-start(f32[64,3072]{1,0:T(8,128)} %constant_dynamic-slice_fusion.1), channel_id=1, source_target_pairs={{0,16},{8,24},{16,0},{24,8},{1,17},{9,25},{17,1},{25,9},{2,18},{10... | collective-permute-start | bytes 2359304 | tf_op jit(solution)/shard_map/ppermute | solution.py:428
  71.4 0.0 copy-start.1
  71.4 0.8 collective-permute-start.11
  72.9 1.6 %collective-permute-done.13.refs_2_ = f32[64,4096]{1,0:T(8,128)} collective-permute-done((f32[64,4096]{1,0:T(8,128)}, f32[64,4096]{1,0:T(8,128)}, u32[]{:S(2)}, u32[]{:S(2)}) %collective-permute-start.13) | collective-permute-done | bytes 1048608 | tf_op jit(solution)/shard_map/ppermute | solution.py:428
  74.5 19.4 %collective-permute-done.11.refs_1_ = f32[256,128]{1,0:T(8,128)S(1)} collective-permute-done((f32[256,128]{1,0:T(8,128)S(1)}, f32[256,128]{1,0:T(8,128)S(1)}, u32[]{:S(2)}, u32[]{:S(2)}) %collective-permute-start.11) | collective-permute-done | bytes 131104 | tf_op jit(solution)/shard_map/ppermute | solution.py:428
  93.9 0.6 copy-done.2
  94.5 9.5 %small.1.coeffs = f32[64,256]{1,0:T(8,128)} custom-call(s32[1]{0:T(128)} %bitcast.where.me_ref, s32[1]{0:T(128)S(6)} %copy.10.root_ref, s32[4]{0:T(128)} %code_ref.1, f32[256,128]{1,0:T(8,128)} %copy-done.1, f32[256,128]{1,0:T(8,128)} %copy-done.2), custom_call_target="tpu_custom_call" | custom-call | flops 5242880000 | bytes 262144 | tf_op jit(solution)/shard_map/small/pallas_call | solution.py:300
  104.1 6.5 %mix.4.refs_4_ = f32[64,16384]{1,0:T(8,128)} custom-call(s32[1]{0:T(128)} %bitcast.where.me_ref, f32[64,256]{1,0:T(8,128)} %small.1.coeffs, f32[64,16384]{1,0:T(8,128)} %bitcast.16, f32[64,16384]{1,0:T(8,128)} %collective-permute-done.refs_1_, f32[64,4096]{1,0:T(8,128)} %collective-permute-done.4.refs_2_, f32[64,4096]{1,0:T(8,128)} %collective-permute-done.15.refs_3_, ...), custom_call_target="tpu_custom_call" | custom-call | flops 1610612736 | bytes 10485760 | tf_op jit(solution)/shard_map/mix/pallas_call | solution.py:376
  110.6 0.1 collective-permute-start.20
  110.7 1.8 %collective-permute-start.12 = (f32[64,1024]{1,0:T(8,128)}, f32[64,1024]{1,0:T(8,128)}, u32[]{:S(2)}, u32[]{:S(2)}) collective-permute-start(f32[64,1024]{1,0:T(8,128)} %constant_dynamic-slice_fusion), channel_id=1, source_target_pairs={{0,16},{8,24},{16,0},{24,8},{1,17},{9,25},{17,1},{25,9},{2,18},{10... | collective-permute-start | bytes 786440 | tf_op jit(solution)/shard_map/ppermute | solution.py:428
  112.5 4.6 %mix.5.refs_4_ = f32[64,16384]{1,0:T(8,128)} custom-call(s32[1]{0:T(128)} %bitcast.where.me_ref, f32[64,256]{1,0:T(8,128)} %small.1.coeffs, f32[64,16384]{1,0:T(8,128)} %bitcast.17, f32[64,16384]{1,0:T(8,128)} %collective-permute-done.refs_1_, f32[64,4096]{1,0:T(8,128)} %collective-permute-done.13.refs_2_, ...), custom_call_target="tpu_custom_call", output_to_operand_aliasing={{}: (6, {})} | custom-call | flops 805306368 | bytes 5242880 | tf_op jit(solution)/shard_map/mix/pallas_call | solution.py:376
  117.1 2.6 %collective-permute-done.12.refs_2_ = f32[64,1024]{1,0:T(8,128)} collective-permute-done((f32[64,1024]{1,0:T(8,128)}, f32[64,1024]{1,0:T(8,128)}, u32[]{:S(2)}, u32[]{:S(2)}) %collective-permute-start.12) | collective-permute-done | bytes 262176 | tf_op jit(solution)/shard_map/ppermute | solution.py:428
  119.7 4.1 %mix.6.refs_4_ = f32[64,16384]{1,0:T(8,128)} custom-call(s32[1]{0:T(128)} %bitcast.where.me_ref, f32[64,256]{1,0:T(8,128)} %small.1.coeffs, f32[64,16384]{1,0:T(8,128)} %bitcast.18, f32[64,16384]{1,0:T(8,128)} %collective-permute-done.refs_1_, f32[64,3072]{1,0:T(8,128)} %collective-permute-done.19.refs_2_, ...), custom_call_target="tpu_custom_call", output_to_operand_aliasing={{}: (6, {})} | custom-call | flops 603979776 | bytes 3932160 | tf_op jit(solution)/shard_map/mix/pallas_call | solution.py:376
  123.9 3.2 %mix.7 = f32[64,16384]{1,0:T(8,128)} custom-call(s32[1]{0:T(128)} %bitcast.where.me_ref, f32[64,256]{1,0:T(8,128)} %small.1.coeffs, f32[64,16384]{1,0:T(8,128)} %bitcast.19, f32[64,16384]{1,0:T(8,128)} %collective-permute-done.refs_1_, f32[64,1024]{1,0:T(8,128)} %collective-permute-done.12.refs_2_, ...), custom_call_target="tpu_custom_call", output_to_operand_aliasing={{}: (6, {})} | custom-call | flops 201326592 | bytes 1310720 | tf_op jit(solution)/shard_map/mix/pallas_call | solution.py:376
  (26 shorter events, 0.1 us)
Async XLA Ops:
  0.0 12.8 %collective-permute-start = (f32[64,16384]{1,0:T(8,128)}, f32[64,16384]{1,0:T(8,128)}, u32[]{:S(2)}, u32[]{:S(2)}) collective-permute-start(f32[64,16384]{1,0:T(8,128)} %bitcast.6), channel_id=1, source_target_pairs={{0,8},{8,0},{16,24},{24,16},{1,9},{9,1},{17,25},{25,17},{2,10},{10... | collective-permute-start | bytes 12582920 | tf_op jit(solution)/shard_map/ppermute | solution.py:428
  2.8 31.1 %collective-permute-start.4 = (f32[64,4096]{1,0:T(8,128)}, f32[64,4096]{1,0:T(8,128)}, u32[]{:S(2)}, u32[]{:S(2)}) collective-permute-start(f32[64,4096]{1,0:T(8,128)} %dynamic-slice_bitcast_fusion), channel_id=1, source_target_pairs={{0,16},{8,24},{16,0},{24,8},{1,17},{9,25},{17,1},{25,9},{2,18},{10... | collective-permute-start | bytes 3145736 | tf_op jit(solution)/shard_map/ppermute | solution.py:428
  17.9 4.1 %collective-permute-start.1 = (f32[64,128]{1,0:T(8,128)S(1)}, f32[64,128]{1,0:T(8,128)S(1)}, u32[]{:S(2)}, u32[]{:S(2)}) collective-permute-start(f32[64,128]{1,0:T(8,128)S(1)} %pad_maximum_fusion.2), channel_id=1, source_target_pairs={{0,1},{1,0},{2,3},{3,2},{4,5},{5,4},{6,7},{7,6},{8,9},{9,8},{10,11... | collective-permute-start | bytes 98312 | tf_op jit(solution)/shard_map/ppermute | solution.py:436
  21.5 24.9 %collective-permute-start.6 = (f32[64,3072]{1,0:T(8,128)}, f32[64,3072]{1,0:T(8,128)}, u32[]{:S(2)}, u32[]{:S(2)}) collective-permute-start(f32[64,3072]{1,0:T(8,128)} %constant_dynamic-slice_fusion.4), channel_id=1, source_target_pairs={{0,16},{8,24},{16,0},{24,8},{1,17},{9,25},{17,1},{25,9},{2,18},{10... | collective-permute-start | bytes 2359304 | tf_op jit(solution)/shard_map/ppermute | solution.py:428
  22.9 4.8 %collective-permute-start.2 = (f32[64,128]{1,0:T(8,128)S(1)}, f32[64,128]{1,0:T(8,128)S(1)}, u32[]{:S(2)}, u32[]{:S(2)}) collective-permute-start(f32[64,128]{1,0:T(8,128)S(1)} %fusion.2), channel_id=1, source_target_pairs={{0,2},{1,3},{2,0},{3,1},{4,6},{5,7},{6,4},{7,5},{8,10},{9,11},{10,... | collective-permute-start | bytes 98312 | tf_op jit(solution)/shard_map/ppermute | solution.py:436
  26.2 25.9 %collective-permute-start.5 = (f32[64,1024]{1,0:T(8,128)}, f32[64,1024]{1,0:T(8,128)}, u32[]{:S(2)}, u32[]{:S(2)}) collective-permute-start(f32[64,1024]{1,0:T(8,128)} %constant_dynamic-slice_fusion.3), channel_id=1, source_target_pairs={{0,16},{8,24},{16,0},{24,8},{1,17},{9,25},{17,1},{25,9},{2,18},{10... | collective-permute-start | bytes 786440 | tf_op jit(solution)/shard_map/ppermute | solution.py:428
  27.7 5.6 %collective-permute-start.3 = (f32[64,128]{1,0:T(8,128)S(1)}, f32[64,128]{1,0:T(8,128)S(1)}, u32[]{:S(2)}, u32[]{:S(2)}) collective-permute-start(f32[64,128]{1,0:T(8,128)S(1)} %add.62), channel_id=1, source_target_pairs={{0,4},{1,5},{2,6},{3,7},{4,0},{5,1},{6,2},{7,3},{8,12},{9,13},{10,... | collective-permute-start | bytes 98312 | tf_op jit(solution)/shard_map/ppermute | solution.py:436
  32.7 41.8 %collective-permute-start.13 = (f32[64,4096]{1,0:T(8,128)}, f32[64,4096]{1,0:T(8,128)}, u32[]{:S(2)}, u32[]{:S(2)}) collective-permute-start(f32[64,4096]{1,0:T(8,128)} %constant_dynamic-slice_fusion.2), channel_id=1, source_target_pairs={{0,16},{8,24},{16,0},{24,8},{1,17},{9,25},{17,1},{25,9},{2,18},{10... | collective-permute-start | bytes 3145736 | tf_op jit(solution)/shard_map/ppermute | solution.py:428
  45.0 59.1 %collective-permute-start.15 = (f32[64,4096]{1,0:T(8,128)}, f32[64,4096]{1,0:T(8,128)}, u32[]{:S(2)}, u32[]{:S(2)}) collective-permute-start(f32[64,4096]{1,0:T(8,128)} %collective-permute-done.4.refs_2_), channel_id=1, source_target_pairs={{0,8},{8,0},{16,24},{24,16},{1,9},{9,1},{17,25},{25,17},{2,10},{10... | collective-permute-start | bytes 3145736 | tf_op jit(solution)/shard_map/ppermute | solution.py:428
  50.7 18.3 %copy-start = (f32[64,128]{1,0:T(8,128)S(1)}, f32[64,128]{1,0:T(8,128)}, u32[]{:S(2)}) copy-start(f32[64,128]{1,0:T(8,128)} %invert.1) | copy-start | bytes 98308
  55.1 4.2 %collective-permute-start.7 = (f32[64,128]{1,0:T(8,128)}, f32[64,128]{1,0:T(8,128)S(1)}, u32[]{:S(2)}, u32[]{:S(2)}) collective-permute-start(f32[64,128]{1,0:T(8,128)} %shard_map.40), channel_id=1, source_target_pairs={{0,1},{1,0},{2,3},{3,2},{4,5},{5,4},{6,7},{7,6},{8,9},{9,8},{10,11... | collective-permute-start | bytes 98312 | tf_op jit(solution)/shard_map/ppermute | solution.py:436
  60.1 4.0 %collective-permute-start.8 = (f32[64,128]{1,0:T(8,128)S(1)}, f32[64,128]{1,0:T(8,128)S(1)}, u32[]{:S(2)}, u32[]{:S(2)}) collective-permute-start(f32[64,128]{1,0:T(8,128)S(1)} %add.68), channel_id=1, source_target_pairs={{0,2},{1,3},{2,0},{3,1},{4,6},{5,7},{6,4},{7,5},{8,10},{9,11},{10,... | collective-permute-start | bytes 98312 | tf_op jit(solution)/shard_map/ppermute | solution.py:436
  64.0 4.9 %collective-permute-start.9 = (f32[64,128]{1,0:T(8,128)S(1)}, f32[64,128]{1,0:T(8,128)S(1)}, u32[]{:S(2)}, u32[]{:S(2)}) collective-permute-start(f32[64,128]{1,0:T(8,128)S(1)} %add.71), channel_id=1, source_target_pairs={{0,4},{1,5},{2,6},{3,7},{4,0},{5,1},{6,2},{7,3},{8,12},{9,13},{10,... | collective-permute-start | bytes 98312 | tf_op jit(solution)/shard_map/ppermute | solution.py:436
  69.0 2.4 %collective-permute-start.10 = (f32[128,128]{1,0:T(8,128)S(1)}, f32[128,128]{1,0:T(8,128)S(1)}, u32[]{:S(2)}, u32[]{:S(2)}) collective-permute-start(f32[128,128]{1,0:T(8,128)S(1)} %pad_maximum_fusion.1), channel_id=1, source_target_pairs={{0,8},{8,0},{16,24},{24,16},{1,9},{9,1},{17,25},{25,17},{2,10},{10... | collective-permute-start | bytes 196616 | tf_op jit(solution)/shard_map/ppermute | solution.py:428
  69.1 35.0 %collective-permute-start.16 = (f32[64,3072]{1,0:T(8,128)}, f32[64,3072]{1,0:T(8,128)}, u32[]{:S(2)}, u32[]{:S(2)}) collective-permute-start(f32[64,3072]{1,0:T(8,128)} %collective-permute-done.6.refs_2_.refs_4_), channel_id=1, source_target_pairs={{0,8},{8,0},{16,24},{24,16},{1,9},{9,1},{17,25},{25,17},{2,10},{10... | collective-permute-start | bytes 2359304 | tf_op jit(solution)/shard_map/ppermute | solution.py:428
  69.6 41.0 %collective-permute-start.19 = (f32[64,3072]{1,0:T(8,128)}, f32[64,3072]{1,0:T(8,128)}, u32[]{:S(2)}, u32[]{:S(2)}) collective-permute-start(f32[64,3072]{1,0:T(8,128)} %constant_dynamic-slice_fusion.1), channel_id=1, source_target_pairs={{0,16},{8,24},{16,0},{24,8},{1,17},{9,25},{17,1},{25,9},{2,18},{10... | collective-permute-start | bytes 2359304 | tf_op jit(solution)/shard_map/ppermute | solution.py:428
  71.4 22.5 %copy-start.1 = (f32[256,128]{1,0:T(8,128)}, f32[256,128]{1,0:T(8,128)S(1)}, u32[]{:S(2)}) copy-start(f32[256,128]{1,0:T(8,128)S(1)} %pad_maximum_fusion.refs_0_) | copy-start | bytes 393220
  71.4 22.5 %collective-permute-start.11 = (f32[256,128]{1,0:T(8,128)S(1)}, f32[256,128]{1,0:T(8,128)S(1)}, u32[]{:S(2)}, u32[]{:S(2)}) collective-permute-start(f32[256,128]{1,0:T(8,128)S(1)} %pad_maximum_fusion.refs_0_), channel_id=1, source_target_pairs={{0,16},{8,24},{16,0},{24,8},{1,17},{9,25},{17,1},{25,9},{2,18},{10... | collective-permute-start | bytes 393224 | tf_op jit(solution)/shard_map/ppermute | solution.py:428
  74.5 29.5 %collective-permute-start.17 = (f32[64,1024]{1,0:T(8,128)}, f32[64,1024]{1,0:T(8,128)}, u32[]{:S(2)}, u32[]{:S(2)}) collective-permute-start(f32[64,1024]{1,0:T(8,128)} %collective-permute-done.5.refs_2_.refs_6_), channel_id=1, source_target_pairs={{0,8},{8,0},{16,24},{24,16},{1,9},{9,1},{17,25},{25,17},{2,10},{10... | collective-permute-start | bytes 786440 | tf_op jit(solution)/shard_map/ppermute | solution.py:428
  93.9 0.6 copy-start.2
  93.9 18.6 %collective-permute-start.14 = (f32[64,4096]{1,0:T(8,128)}, f32[64,4096]{1,0:T(8,128)}, u32[]{:S(2)}, u32[]{:S(2)}) collective-permute-start(f32[64,4096]{1,0:T(8,128)} %collective-permute-done.13.refs_2_), channel_id=1, source_target_pairs={{0,8},{8,0},{16,24},{24,16},{1,9},{9,1},{17,25},{25,17},{2,10},{10... | collective-permute-start | bytes 3145736 | tf_op jit(solution)/shard_map/ppermute | solution.py:428
  110.6 9.1 %collective-permute-start.20 = (f32[64,3072]{1,0:T(8,128)}, f32[64,3072]{1,0:T(8,128)}, u32[]{:S(2)}, u32[]{:S(2)}) collective-permute-start(f32[64,3072]{1,0:T(8,128)} %collective-permute-done.19.refs_2_), channel_id=1, source_target_pairs={{0,8},{8,0},{16,24},{24,16},{1,9},{9,1},{17,25},{25,17},{2,10},{10... | collective-permute-start | bytes 2359304 | tf_op jit(solution)/shard_map/ppermute | solution.py:428
  110.7 9.0 %collective-permute-start.12 = (f32[64,1024]{1,0:T(8,128)}, f32[64,1024]{1,0:T(8,128)}, u32[]{:S(2)}, u32[]{:S(2)}) collective-permute-start(f32[64,1024]{1,0:T(8,128)} %constant_dynamic-slice_fusion), channel_id=1, source_target_pairs={{0,16},{8,24},{16,0},{24,8},{1,17},{9,25},{17,1},{25,9},{2,18},{10... | collective-permute-start | bytes 786440 | tf_op jit(solution)/shard_map/ppermute | solution.py:428
  119.7 4.2 %collective-permute-start.18 = (f32[64,1024]{1,0:T(8,128)}, f32[64,1024]{1,0:T(8,128)}, u32[]{:S(2)}, u32[]{:S(2)}) collective-permute-start(f32[64,1024]{1,0:T(8,128)} %collective-permute-done.12.refs_2_), channel_id=1, source_target_pairs={{0,8},{8,0},{16,24},{24,16},{1,9},{9,1},{17,25},{25,17},{2,10},{10... | collective-permute-start | bytes 786440 | tf_op jit(solution)/shard_map/ppermute | solution.py:428
